TPU v7x, 32 devices: a whole 2x2x4 slice. The times are simulated.
32 devices in a mesh: dev: 32 (over z, y, x, core).
Axes of the slice: x: 2, y: 2, z: 4, core: 2. Of those that a mesh axis runs over, the one named last changes fastest.
Arguments:
- gauss_params: float32 [59, 262144], P(None, 'dev'), may hold values from -8 to 8, as said below
- adam_first: float32 [59, 262144], P(None, 'dev'), may hold values from -6 to 6
- adam_second: float32 [59, 262144], P(None, 'dev'), may hold values from 0.0001 to 100
- camera: float32 [2, 6], replicated, may hold values from -0.004 to 0.004
- send_first: int32 [32, 4096], P('dev'), may hold values from -1 to 8191, as said below
- send_second: int32 [32, 4096], P('dev'), may hold values from -1 to 8191, as said below
- lists_first: int32 [1024, 128], P('dev'), may hold values from -1 to 4095, as said below
- lists_second: int32 [1024, 128], P('dev'), may hold values from -1 to 4095, as said below
- tiles_first: int32 [1024], P('dev'), may hold values from 0 to 1023, as said below
- tiles_second: int32 [1024], P('dev'), may hold values from 0 to 1023, as said below
- targets: float32 [1024, 3, 256], P('dev'), may hold values from 0 to 1
Outputs:
- new_params: float32 [59, 262144], P(None, 'dev')
- new_first: float32 [59, 262144], P(None, 'dev')
- new_second: float32 [59, 262144], P(None, 'dev')
- rendered_next: float32 [1024, 3, 256], P('dev')
Inputs may be any that keep to these rules, and one draw needn't show every extreme that they name: `gauss_params`: rows 0 to 2 hold a position, 3 to 5 log scales, 6 to 9 a quaternion (w, x, y, z) with w at least 1, 10 an opacity logit, 11 + 16 c + k the spherical-harmonic coefficient k of colour c. Every Gaussian lies at depth 1.4 or more in front of both cameras. `send_first`: row s holds, for each destination d in turn, 128 slots: local column indices of Gaussians of device s, the used ones first, then -1. Entries other than -1 in a row are distinct. Some destination gets 128 used slots from every device. `send_second`: same form as send_first, but unused slots (-1) may stand anywhere in a destination's run. Some destination gets 128 used slots from every device. `lists_first`: row r, rendered by device r // 32, lists in compositing order (front first) received slots s * 128 + k of that device (slot k from device s), only used slots, then -1 to the end. Every used slot of a device appears exactly once among its rows. Some rows have no -1. `lists_second`: same form as lists_first, for the next view and its send array. `tiles_first`: A permutation of the image's tiles. `tiles_second`: A permutation of the image's tiles.
All inputs are finite; a program needn't handle non-finite values.
Results may differ from a plain program's by a relative error of at most 0.0003.
Values sent between devices are 32-bit elements; how exact they have to be, the bound alone decides.
No kernel may reach another device: no remote copies, remote signals or barrier semaphores. Data moves between devices by JAX's collectives and lax.ppermute only.
A program may use at most 128 MiB of HBM per device.

v0:
```python
import jax
import jax.numpy as jnp
import numpy as np
from jax import lax
from jax.sharding import PartitionSpec as P

LIST_LEN = 128
TILE_PIXELS = 256
TILES_X = 128


tile_edge = 16
focal_length = 1000.0
blur_floor = 0.3
adam_epsilon = 1e-08
bias_first = 1.0 - 0.9**20
bias_second = 1.0 - 0.999**20
sh_first = 0.28209479177387814
sh_second = 0.4886025119029199
sh_third = (
    1.0925484305920792,
    -1.0925484305920792,
    0.31539156525252005,
    -1.0925484305920792,
    0.5462742152960396,
)
sh_fourth = (
    -0.5900435899266435,
    2.890611442640554,
    -0.4570457994644658,
    0.3731763325901154,
    -0.4570457994644658,
    1.445305721320277,
    -0.5900435899266435,
)


def rate_values():
    values = np.full((59,), 0.000125)
    values[0:3] = 0.00016
    values[3:6] = 0.005
    values[6:10] = 0.001
    values[10] = 0.05
    values[11] = 0.0025
    values[27] = 0.0025
    values[43] = 0.0025
    return values


def camera_frame(camera_row):
    cosine_a, sine_a = (jnp.cos(camera_row[0]), jnp.sin(camera_row[0]))
    cosine_b, sine_b = (jnp.cos(camera_row[1]), jnp.sin(camera_row[1]))
    cosine_c, sine_c = (jnp.cos(camera_row[2]), jnp.sin(camera_row[2]))
    filler_zero = jnp.zeros_like(cosine_a)
    filler_one = jnp.ones_like(cosine_a)
    turn_x = jnp.stack(
        [
            jnp.stack([filler_one, filler_zero, filler_zero]),
            jnp.stack([filler_zero, cosine_a, -sine_a]),
            jnp.stack([filler_zero, sine_a, cosine_a]),
        ]
    )
    turn_y = jnp.stack(
        [
            jnp.stack([cosine_b, filler_zero, sine_b]),
            jnp.stack([filler_zero, filler_one, filler_zero]),
            jnp.stack([-sine_b, filler_zero, cosine_b]),
        ]
    )
    turn_z = jnp.stack(
        [
            jnp.stack([cosine_c, -sine_c, filler_zero]),
            jnp.stack([sine_c, cosine_c, filler_zero]),
            jnp.stack([filler_zero, filler_zero, filler_one]),
        ]
    )
    highest = lax.Precision.HIGHEST
    rotation = jnp.dot(turn_z, jnp.dot(turn_y, turn_x, precision=highest), precision=highest)
    return (rotation, camera_row[3:6])


def sh_terms(along_x, along_y, along_z):
    square_x, square_y, square_z = (along_x * along_x, along_y * along_y, along_z * along_z)
    return [
        -sh_second * along_y,
        sh_second * along_z,
        -sh_second * along_x,
        sh_third[0] * along_x * along_y,
        sh_third[1] * along_y * along_z,
        sh_third[2] * (2.0 * square_z - square_x - square_y),
        sh_third[3] * along_x * along_z,
        sh_third[4] * (square_x - square_y),
        sh_fourth[0] * along_y * (3.0 * square_x - square_y),
        sh_fourth[1] * along_x * along_y * along_z,
        sh_fourth[2] * along_y * (4.0 * square_z - square_x - square_y),
        sh_fourth[3] * along_z * (2.0 * square_z - 3.0 * square_x - 3.0 * square_y),
        sh_fourth[4] * along_x * (4.0 * square_z - square_x - square_y),
        sh_fourth[5] * along_z * (square_x - square_y),
        sh_fourth[6] * along_x * (square_x - 3.0 * square_y),
    ]


def project(params, camera_row, image_width, image_height):
    rotation, offset = camera_frame(camera_row)
    centres = params[0:3]
    viewed = [
        rotation[row_index, 0] * centres[0]
        + rotation[row_index, 1] * centres[1]
        + rotation[row_index, 2] * centres[2]
        + offset[row_index]
        for row_index in range(3)
    ]
    inverse_depth = 1.0 / viewed[2]
    screen_u = focal_length * viewed[0] * inverse_depth + 0.5 * image_width
    screen_v = focal_length * viewed[1] * inverse_depth + 0.5 * image_height
    scales = jnp.exp(params[3:6])
    versor = params[6:10] / jnp.sqrt(jnp.sum(params[6:10] * params[6:10], axis=0))
    part_w, part_x, part_y, part_z = (versor[0], versor[1], versor[2], versor[3])
    turn_rows = [
        [
            1.0 - 2.0 * (part_y * part_y + part_z * part_z),
            2.0 * (part_x * part_y - part_w * part_z),
            2.0 * (part_x * part_z + part_w * part_y),
        ],
        [
            2.0 * (part_x * part_y + part_w * part_z),
            1.0 - 2.0 * (part_x * part_x + part_z * part_z),
            2.0 * (part_y * part_z - part_w * part_x),
        ],
        [
            2.0 * (part_x * part_z - part_w * part_y),
            2.0 * (part_y * part_z + part_w * part_x),
            1.0 - 2.0 * (part_x * part_x + part_y * part_y),
        ],
    ]
    factor = [
        [turn_rows[row_index][col_index] * scales[col_index] for col_index in range(3)]
        for row_index in range(3)
    ]
    spread = [
        [
            factor[row_index][0] * factor[col_index][0]
            + factor[row_index][1] * factor[col_index][1]
            + factor[row_index][2] * factor[col_index][2]
            for col_index in range(3)
        ]
        for row_index in range(3)
    ]
    jacobian = [
        [
            focal_length * inverse_depth,
            0.0,
            -focal_length * viewed[0] * inverse_depth * inverse_depth,
        ],
        [
            0.0,
            focal_length * inverse_depth,
            -focal_length * viewed[1] * inverse_depth * inverse_depth,
        ],
    ]
    mapping = [
        [
            jacobian[row_index][0] * rotation[0, col_index]
            + jacobian[row_index][1] * rotation[1, col_index]
            + jacobian[row_index][2] * rotation[2, col_index]
            for col_index in range(3)
        ]
        for row_index in range(2)
    ]

    def mapped(first_index, second_index):
        running = 0.0
        for inner_a in range(3):
            for inner_b in range(3):
                running = (
                    running
                    + mapping[first_index][inner_a]
                    * spread[inner_a][inner_b]
                    * mapping[second_index][inner_b]
                )
        return running

    cover_a = mapped(0, 0) + blur_floor
    cover_b = mapped(0, 1)
    cover_c = mapped(1, 1) + blur_floor
    determinant = cover_a * cover_c - cover_b * cover_b
    opacity = jax.nn.sigmoid(params[10])
    centre_cam = [
        -(
            rotation[0, col_index] * offset[0]
            + rotation[1, col_index] * offset[1]
            + rotation[2, col_index] * offset[2]
        )
        for col_index in range(3)
    ]
    towards = [centres[col_index] - centre_cam[col_index] for col_index in range(3)]
    length = jnp.sqrt(towards[0] * towards[0] + towards[1] * towards[1] + towards[2] * towards[2])
    harmonics = sh_terms(towards[0] / length, towards[1] / length, towards[2] / length)
    colours = []
    for channel in range(3):
        running = 0.5 + sh_first * params[11 + 16 * channel]
        for term_index in range(1, 16):
            running = running + harmonics[term_index - 1] * params[11 + 16 * channel + term_index]
        colours.append(jnp.maximum(running, 0.0))
    return jnp.stack(
        [
            screen_u,
            screen_v,
            cover_c / determinant,
            -cover_b / determinant,
            cover_a / determinant,
            opacity,
        ]
        + colours
    )


def composite(gathered, live_mask, tile_numbers, triangle):
    pixel_ids = jnp.arange(TILE_PIXELS, dtype=jnp.int32)
    pixel_col = (tile_numbers % TILES_X)[:, None] * tile_edge + pixel_ids[None, :] % tile_edge
    pixel_row = (tile_numbers // TILES_X)[:, None] * tile_edge + pixel_ids[None, :] // tile_edge
    offset_x = gathered[0][:, None, :] - (pixel_col.astype(gathered.dtype) + 0.5)[:, :, None]
    offset_y = gathered[1][:, None, :] - (pixel_row.astype(gathered.dtype) + 0.5)[:, :, None]
    exponent = (
        -0.5
        * (
            gathered[2][:, None, :] * offset_x * offset_x
            + gathered[4][:, None, :] * offset_y * offset_y
        )
        - gathered[3][:, None, :] * offset_x * offset_y
    )
    coverage = gathered[5][:, None, :] * jnp.exp(exponent) * live_mask[:, None, :]
    log_clear = jnp.log1p(-coverage)
    before = jnp.einsum("bpj,ji->bpi", log_clear, triangle, precision=lax.Precision.HIGHEST)
    weight = coverage * jnp.exp(before)
    return jnp.einsum("bpi,cbi->bcp", weight, gathered[6:9], precision=lax.Precision.HIGHEST)


def group_of():
    return 8


def selector(width, ids, dtype):
    return (jnp.arange(width, dtype=jnp.int32)[:, None] == ids[None, :]).astype(dtype)


def block_inputs(buffer, tile_lists):
    live_mask = (tile_lists >= 0).astype(buffer.dtype)
    safe_ids = jnp.maximum(tile_lists, 0).reshape(-1)
    choose = selector(buffer.shape[1], safe_ids, buffer.dtype)
    gathered = jnp.dot(buffer, choose, precision=lax.Precision.HIGHEST).reshape(
        buffer.shape[0], tile_lists.shape[0], LIST_LEN
    )
    return (gathered, live_mask, choose)


def train_tiles(buffer, tile_lists, tile_numbers, targets, triangle):
    tile_group = group_of()
    block_count = tile_lists.shape[0] // tile_group

    def train_one_block(running, pieces):
        piece_lists, piece_tiles, piece_targets = pieces
        gathered, live_mask, choose = block_inputs(buffer, piece_lists)

        def block_loss(splat_block):
            rendered = composite(splat_block, live_mask, piece_tiles, triangle)
            return 0.5 * jnp.sum((rendered - piece_targets) ** 2)

        splat_grad = jax.grad(block_loss)(gathered) * live_mask[None, :, :]
        splat_grad = splat_grad.reshape(buffer.shape[0], tile_group * LIST_LEN)
        return (
            running
            + lax.dot_general(
                splat_grad, choose, (((1,), (1,)), ((), ())), precision=lax.Precision.HIGHEST
            ),
            None,
        )

    pieces = (
        tile_lists.reshape(block_count, tile_group, LIST_LEN),
        tile_numbers.reshape(block_count, tile_group),
        targets.reshape(block_count, tile_group, 3, TILE_PIXELS),
    )
    running, unused = lax.scan(train_one_block, jnp.zeros(buffer.shape, buffer.dtype), pieces)
    return running


def render_tiles(buffer, tile_lists, tile_numbers, triangle):
    tile_group = group_of()
    block_count = tile_lists.shape[0] // tile_group

    def render_one_block(pieces):
        piece_lists, piece_tiles = pieces
        gathered, live_mask, choose = block_inputs(buffer, piece_lists)
        return composite(gathered, live_mask, piece_tiles, triangle)

    rendered = lax.map(
        render_one_block,
        (
            tile_lists.reshape(block_count, tile_group, LIST_LEN),
            tile_numbers.reshape(block_count, tile_group),
        ),
    )
    return rendered.reshape(tile_lists.shape[0], 3, TILE_PIXELS)


def slot_group():
    return 512


def pick_slots(source, slots):
    width = slot_group()
    blocks = slots.shape[0] // width
    safe_ids = jnp.maximum(slots, 0).reshape(blocks, width)

    def pick_one_block(block_ids):
        return jnp.dot(
            source,
            selector(source.shape[1], block_ids, source.dtype),
            precision=lax.Precision.HIGHEST,
        )

    picked = lax.map(pick_one_block, safe_ids)
    return jnp.transpose(picked, (1, 0, 2)).reshape(source.shape[0], slots.shape[0])


def return_slots(values, slots, local_count):
    width = slot_group()
    blocks = slots.shape[0] // width
    live = (slots >= 0).astype(values.dtype)
    masked = jnp.transpose(
        (values * live[None, :]).reshape(values.shape[0], blocks, width), (1, 0, 2)
    )
    safe_ids = jnp.maximum(slots, 0).reshape(blocks, width)

    def return_one_block(running, pieces):
        block_values, block_ids = pieces
        choose = selector(local_count, block_ids, values.dtype)
        return (
            running
            + lax.dot_general(
                block_values, choose, (((1,), (1,)), ((), ())), precision=lax.Precision.HIGHEST
            ),
            None,
        )

    total, unused = lax.scan(
        return_one_block,
        jnp.zeros((values.shape[0], local_count), values.dtype),
        (masked, safe_ids),
    )
    return total


def shards(
    gauss_params,
    adam_first,
    adam_second,
    camera,
    send_first,
    send_second,
    lists_first,
    lists_second,
    tiles_first,
    tiles_second,
    targets,
):
    devices = lax.axis_size("dev")
    image_width = TILES_X * tile_edge * 1.0
    image_height = lists_first.shape[0] * devices // TILES_X * tile_edge * 1.0
    local_count = gauss_params.shape[1]
    triangle = (jnp.arange(LIST_LEN)[:, None] < jnp.arange(LIST_LEN)[None, :]).astype(
        gauss_params.dtype
    )
    slots_first = send_first[0]
    picked = pick_slots(gauss_params, slots_first)

    def view_first(chosen):
        return project(chosen, camera[0], image_width, image_height)

    arrived = lax.all_to_all(picked, "dev", split_axis=1, concat_axis=1, tiled=True)
    buffer, pullback = jax.vjp(view_first, arrived)
    splat_grads = train_tiles(buffer, lists_first, tiles_first, targets, triangle)
    slot_grads = lax.all_to_all(
        pullback(splat_grads)[0], "dev", split_axis=1, concat_axis=1, tiled=True
    )
    gradient = return_slots(slot_grads, slots_first, local_count)
    new_first = 0.9 * adam_first + 0.1 * gradient
    new_second = 0.999 * adam_second + 0.001 * gradient * gradient
    step_sizes = jnp.asarray(rate_values(), gauss_params.dtype)[:, None]
    new_params = gauss_params - step_sizes * (new_first / bias_first) / (
        jnp.sqrt(new_second / bias_second) + adam_epsilon
    )
    picked_next = pick_slots(new_params, send_second[0])
    buffer_next = project(
        lax.all_to_all(picked_next, "dev", split_axis=1, concat_axis=1, tiled=True),
        camera[1],
        image_width,
        image_height,
    )
    rendered_next = render_tiles(buffer_next, lists_second, tiles_second, triangle)
    return (new_params, new_first, new_second, rendered_next)


def solution(mesh):
    placed = (
        P(None, "dev"),
        P(None, "dev"),
        P(None, "dev"),
        P(),
        P("dev", None),
        P("dev", None),
        P("dev", None),
        P("dev", None),
        P("dev"),
        P("dev"),
        P("dev", None, None),
    )
    return jax.shard_map(
        shards,
        mesh=mesh,
        in_specs=placed,
        out_specs=(P(None, "dev"), P(None, "dev"), P(None, "dev"), P("dev", None, None)),
        check_vma=False,
    )
```

profile of v0, /device:TPU:0, one launch (start us, length us, event | category | flops | bytes accessed | tf_op | source)
XLA Modules:
  0.0 493.7 jit_solution(3253605575347814456)
XLA Ops:
  1.6 60.9 %while.60 = (s32[]{:T(128)}, f32[8,59,512]{2,1,0:T(8,128)S(1)}, s32[8,512]{1,0:T(8,128)S(1)}, f32[59,8192]{1,0:T(8,128)}, s32[]{:T(128)}) while((s32[]{:T(128)}, f32[8,59,512]{2,1,0:T(8,128)S(1)}, s32[8,512]{1,0:T(8,128)S(1)}, f32[59,8192]{1,0:T(8,128)}, s32[]{:T(128)}) %tuple.414), condition=%wide.region_1.2_spmd, body=%wide.region_0.1_spmd.sunk | while | flops 2973761536 | bytes 2070597 | solution.py:323
  9.2 7.6 %fusion.409 = f32[8,59,512]{2,1,0:T(8,128)S(1)} fusion(f32[8,59,512]{2,1,0:T(8,128)S(1)} %get-tuple-element.1000, s32[]{:T(128)} %get-tuple-element.999, f32[59,8192]{1,0:T(8,128)} %get-tuple-element.1007, s32[512]{0:T(512)S(1)} %bitcast.1571), kind=kOutput, calls=%fused_computation.6.clone.1 | convolution fusion | flops 2973761536 | bytes 2066436 | tf_op jit(solution)/shard_map/while/body/eval_jaxpr/dot_general | solution.py:317
  110.5 94.4 %while.64 = (s32[]{:T(128)}, f32[9,4096]{1,0:T(8,128)S(1)}, s32[4,8,128]{2,1,0:T(8,128)S(1)}, f32[9,4096]{1,0:T(8,128)S(1)}, s32[4,8]{1,0:T(4,128)S(1)}, /*index...) while((s32[]{:T(128)}, f32[9,4096]{1,0:T(8,128)S(1)}, ...), condition=%wide.region_10.11_spmd.clone.clone, body=%wide.region_3.10_spmd.clone.clone.sunk | while | flops 1775461632 | bytes 7651711 | solution.py:284
  232.2 26.1 %all-to-all-done.1 = f32[59,32,128]{2,0,1:T(8,128)S(1)} async-done(((f32[59,32,128]{2,0,1:T(8,128)}), f32[59,32,128]{2,0,1:T(8,128)S(1)}, u32[]{:S(2)}, u32[]{:S(2)}) %all-to-all-start.1) | async-done | bytes 966688 | tf_op jit(solution)/shard_map/all_to_all | solution.py:384
  259.1 86.1 %while.63 = (s32[]{:T(128)}, f32[59,8192]{1,0:T(8,128)}, f32[8,59,512]{2,0,1:T(8,128)S(1)}, s32[8,512]{1,0:T(8,128)S(1)}, s32[]{:T(128)}, /*index=5*/s32[]{:T(128)}) while((s32[]{:T(128)}, f32[59,8192]{1,0:T(8,128)}, f32[8,59,512]{2,0,1:T(8,128)S(1)}, s32[8,512]{1,0:T(8,128)S(1)}, s32[]{:T(128)}, /*index=5*/s32[]{:T(128)}) %tuple.432), condition=%wide.region_13.14_spmd.clone, body=%wide.region_12.13_spmd.clone.sunk | while | flops 2974728192 | bytes 4235351 | solution.py:347
  259.3 9.6 %fusion.421 = f32[59,8192]{1,0:T(8,128)} fusion(s32[512]{0:T(512)S(1)} %bitcast.1570, f32[59,8192]{1,0:T(8,128)} %get-tuple-element.1043, pred[]{:T(512)S(6)} %compare.133, f32[1,59,512]{2,0,1:T(1,128)S(1)} %constant_dynamic-slice_fusion.13), kind=kOutput, calls=%fused_computation.72.clone.1 | convolution fusion | flops 2974728192 | bytes 3989505 | tf_op jit(solution)/shard_map/while/body/eval_jaxpr/dot_general | solution.py:341
  269.0 10.8 %fusion.421 = f32[59,8192]{1,0:T(8,128)} fusion(s32[512]{0:T(512)S(1)} %bitcast.1570, f32[59,8192]{1,0:T(8,128)} %get-tuple-element.1043, pred[]{:T(512)S(6)} %compare.133, f32[1,59,512]{2,0,1:T(1,128)S(1)} %constant_dynamic-slice_fusion.13), kind=kOutput, calls=%fused_computation.72.clone.1 | convolution fusion | flops 2974728192 | bytes 3989505 | tf_op jit(solution)/shard_map/while/body/eval_jaxpr/dot_general | solution.py:341
  279.9 10.8 %fusion.421 = f32[59,8192]{1,0:T(8,128)} fusion(s32[512]{0:T(512)S(1)} %bitcast.1570, f32[59,8192]{1,0:T(8,128)} %get-tuple-element.1043, pred[]{:T(512)S(6)} %compare.133, f32[1,59,512]{2,0,1:T(1,128)S(1)} %constant_dynamic-slice_fusion.13), kind=kOutput, calls=%fused_computation.72.clone.1 | convolution fusion | flops 2974728192 | bytes 3989505 | tf_op jit(solution)/shard_map/while/body/eval_jaxpr/dot_general | solution.py:341
  290.8 10.8 %fusion.421 = f32[59,8192]{1,0:T(8,128)} fusion(s32[512]{0:T(512)S(1)} %bitcast.1570, f32[59,8192]{1,0:T(8,128)} %get-tuple-element.1043, pred[]{:T(512)S(6)} %compare.133, f32[1,59,512]{2,0,1:T(1,128)S(1)} %constant_dynamic-slice_fusion.13), kind=kOutput, calls=%fused_computation.72.clone.1 | convolution fusion | flops 2974728192 | bytes 3989505 | tf_op jit(solution)/shard_map/while/body/eval_jaxpr/dot_general | solution.py:341
  301.7 10.8 %fusion.421 = f32[59,8192]{1,0:T(8,128)} fusion(s32[512]{0:T(512)S(1)} %bitcast.1570, f32[59,8192]{1,0:T(8,128)} %get-tuple-element.1043, pred[]{:T(512)S(6)} %compare.133, f32[1,59,512]{2,0,1:T(1,128)S(1)} %constant_dynamic-slice_fusion.13), kind=kOutput, calls=%fused_computation.72.clone.1 | convolution fusion | flops 2974728192 | bytes 3989505 | tf_op jit(solution)/shard_map/while/body/eval_jaxpr/dot_general | solution.py:341
  312.7 10.8 %fusion.421 = f32[59,8192]{1,0:T(8,128)} fusion(s32[512]{0:T(512)S(1)} %bitcast.1570, f32[59,8192]{1,0:T(8,128)} %get-tuple-element.1043, pred[]{:T(512)S(6)} %compare.133, f32[1,59,512]{2,0,1:T(1,128)S(1)} %constant_dynamic-slice_fusion.13), kind=kOutput, calls=%fused_computation.72.clone.1 | convolution fusion | flops 2974728192 | bytes 3989505 | tf_op jit(solution)/shard_map/while/body/eval_jaxpr/dot_general | solution.py:341
  323.6 10.8 %fusion.421 = f32[59,8192]{1,0:T(8,128)} fusion(s32[512]{0:T(512)S(1)} %bitcast.1570, f32[59,8192]{1,0:T(8,128)} %get-tuple-element.1043, pred[]{:T(512)S(6)} %compare.133, f32[1,59,512]{2,0,1:T(1,128)S(1)} %constant_dynamic-slice_fusion.13), kind=kOutput, calls=%fused_computation.72.clone.1 | convolution fusion | flops 2974728192 | bytes 3989505 | tf_op jit(solution)/shard_map/while/body/eval_jaxpr/dot_general | solution.py:341
  334.5 10.8 %fusion.421 = f32[59,8192]{1,0:T(8,128)} fusion(s32[512]{0:T(512)S(1)} %bitcast.1570, f32[59,8192]{1,0:T(8,128)} %get-tuple-element.1043, pred[]{:T(512)S(6)} %compare.133, f32[1,59,512]{2,0,1:T(1,128)S(1)} %constant_dynamic-slice_fusion.13), kind=kOutput, calls=%fused_computation.72.clone.1 | convolution fusion | flops 2974728192 | bytes 3989505 | tf_op jit(solution)/shard_map/while/body/eval_jaxpr/dot_general | solution.py:341
  351.7 60.9 %while.61 = (s32[]{:T(128)}, f32[8,59,512]{2,1,0:T(8,128)S(1)}, s32[8,512]{1,0:T(8,128)S(1)}, f32[59,8192]{1,0:T(8,128)}, s32[]{:T(128)}) while((s32[]{:T(128)}, f32[8,59,512]{2,1,0:T(8,128)S(1)}, s32[8,512]{1,0:T(8,128)S(1)}, f32[59,8192]{1,0:T(8,128)}, s32[]{:T(128)}) %tuple.423), condition=%wide.region_15.16_spmd, body=%wide.region_14.15_spmd.sunk | while | flops 2973761536 | bytes 2070597 | solution.py:323
  351.8 7.6 %fusion.411 = f32[8,59,512]{2,1,0:T(8,128)S(1)} fusion(f32[8,59,512]{2,1,0:T(8,128)S(1)} %get-tuple-element.1060, s32[]{:T(128)} %get-tuple-element.1059, f32[59,8192]{1,0:T(8,128)} %get-tuple-element.1067, s32[512]{0:T(512)S(1)} %bitcast.1572), kind=kOutput, calls=%fused_computation.12.clone.1 | convolution fusion | flops 2973761536 | bytes 2066436 | tf_op jit(solution)/shard_map/while/body/eval_jaxpr/dot_general | solution.py:317
  359.4 7.6 %fusion.411 = f32[8,59,512]{2,1,0:T(8,128)S(1)} fusion(f32[8,59,512]{2,1,0:T(8,128)S(1)} %get-tuple-element.1060, s32[]{:T(128)} %get-tuple-element.1059, f32[59,8192]{1,0:T(8,128)} %get-tuple-element.1067, s32[512]{0:T(512)S(1)} %bitcast.1572), kind=kOutput, calls=%fused_computation.12.clone.1 | convolution fusion | flops 2973761536 | bytes 2066436 | tf_op jit(solution)/shard_map/while/body/eval_jaxpr/dot_general | solution.py:317
  367.0 7.6 %fusion.411 = f32[8,59,512]{2,1,0:T(8,128)S(1)} fusion(f32[8,59,512]{2,1,0:T(8,128)S(1)} %get-tuple-element.1060, s32[]{:T(128)} %get-tuple-element.1059, f32[59,8192]{1,0:T(8,128)} %get-tuple-element.1067, s32[512]{0:T(512)S(1)} %bitcast.1572), kind=kOutput, calls=%fused_computation.12.clone.1 | convolution fusion | flops 2973761536 | bytes 2066436 | tf_op jit(solution)/shard_map/while/body/eval_jaxpr/dot_general | solution.py:317
  374.6 7.6 %fusion.411 = f32[8,59,512]{2,1,0:T(8,128)S(1)} fusion(f32[8,59,512]{2,1,0:T(8,128)S(1)} %get-tuple-element.1060, s32[]{:T(128)} %get-tuple-element.1059, f32[59,8192]{1,0:T(8,128)} %get-tuple-element.1067, s32[512]{0:T(512)S(1)} %bitcast.1572), kind=kOutput, calls=%fused_computation.12.clone.1 | convolution fusion | flops 2973761536 | bytes 2066436 | tf_op jit(solution)/shard_map/while/body/eval_jaxpr/dot_general | solution.py:317
  382.2 7.6 %fusion.411 = f32[8,59,512]{2,1,0:T(8,128)S(1)} fusion(f32[8,59,512]{2,1,0:T(8,128)S(1)} %get-tuple-element.1060, s32[]{:T(128)} %get-tuple-element.1059, f32[59,8192]{1,0:T(8,128)} %get-tuple-element.1067, s32[512]{0:T(512)S(1)} %bitcast.1572), kind=kOutput, calls=%fused_computation.12.clone.1 | convolution fusion | flops 2973761536 | bytes 2066436 | tf_op jit(solution)/shard_map/while/body/eval_jaxpr/dot_general | solution.py:317
  389.8 7.6 %fusion.411 = f32[8,59,512]{2,1,0:T(8,128)S(1)} fusion(f32[8,59,512]{2,1,0:T(8,128)S(1)} %get-tuple-element.1060, s32[]{:T(128)} %get-tuple-element.1059, f32[59,8192]{1,0:T(8,128)} %get-tuple-element.1067, s32[512]{0:T(512)S(1)} %bitcast.1572), kind=kOutput, calls=%fused_computation.12.clone.1 | convolution fusion | flops 2973761536 | bytes 2066436 | tf_op jit(solution)/shard_map/while/body/eval_jaxpr/dot_general | solution.py:317
  397.5 7.6 %fusion.411 = f32[8,59,512]{2,1,0:T(8,128)S(1)} fusion(f32[8,59,512]{2,1,0:T(8,128)S(1)} %get-tuple-element.1060, s32[]{:T(128)} %get-tuple-element.1059, f32[59,8192]{1,0:T(8,128)} %get-tuple-element.1067, s32[512]{0:T(512)S(1)} %bitcast.1572), kind=kOutput, calls=%fused_computation.12.clone.1 | convolution fusion | flops 2973761536 | bytes 2066436 | tf_op jit(solution)/shard_map/while/body/eval_jaxpr/dot_general | solution.py:317
  405.1 7.6 %fusion.411 = f32[8,59,512]{2,1,0:T(8,128)S(1)} fusion(f32[8,59,512]{2,1,0:T(8,128)S(1)} %get-tuple-element.1060, s32[]{:T(128)} %get-tuple-element.1059, f32[59,8192]{1,0:T(8,128)} %get-tuple-element.1067, s32[512]{0:T(512)S(1)} %bitcast.1572), kind=kOutput, calls=%fused_computation.12.clone.1 | convolution fusion | flops 2973761536 | bytes 2066436 | tf_op jit(solution)/shard_map/while/body/eval_jaxpr/dot_general | solution.py:317
  445.0 7.6 %broadcast_multiply_fusion.1 = (f32[1,32,128]{2,1,0:T(8,128)S(1)}, f32[1,32,128]{2,1,0:T(8,128)S(1)}, f32[1,32,128]{2,1,0:T(8,128)S(1)}, f32[1,32,128]{2,1,0:T(8...) fusion(f32[]{:T(128)} %bitcast.132, ...), kind=kLoop, calls=%fused_computation.627 | loop fusion | flops 98304 | bytes 180284 | tf_op jit(solution)/shard_map/mul | solution.py:158
  457.4 36.0 %while.62 = (s32[]{:T(128)}, f32[4,8,3,256]{3,1,0,2:T(8,128)}, s32[4,8,128]{2,1,0:T(8,128)S(1)}, f32[9,4096]{1,0:T(8,128)S(1)}, s32[4,8]{1,0:T(4,128)S(1)}, /*index=5*/s32[]{:T(128)}) while((s32[]{:T(128)}, f32[4,8,3,256]{3,1,0,2:T(8,128)}, s32[4,8,128]{2,1,0:T(8,128)S(1)}, f32[9,4096]{1,0:T(8,128)S(1)}, s32[4,8]{1,0:T(4,128)S(1)}, ...), condition=%wide.region_18.19_spmd.clone, body=%wide.region_17.18_spmd.clone.sunk | while | flops 876660928 | bytes 2507605 | solution.py:297
  (295 shorter events, 256.8 us)
Async XLA Ops:
  63.1 8.9 %copy-start.5 = (f32[2,6]{1,0:T(2,128)S(1)}, f32[2,6]{1,0:T(2,128)}, u32[]{:S(2)}) copy-start(f32[2,6]{1,0:T(2,128)} %param.25) | copy-start | bytes 148
  63.2 14.1 %copy-start.10 = (f32[1,3]{1,0:T(1,128)S(1)}, f32[1,3]{1,0:T(1,128)}, u32[]{:S(2)}) copy-start(f32[1,3]{1,0:T(1,128)} %constant.324.clone.1) | copy-start | bytes 40
  63.2 14.1 %copy-start.11 = (f32[1,3]{1,0:T(1,128)S(1)}, f32[1,3]{1,0:T(1,128)}, u32[]{:S(2)}) copy-start(f32[1,3]{1,0:T(1,128)} %constant.325.clone.1) | copy-start | bytes 40
  63.2 14.2 %copy-start.6 = (f32[1,3]{1,0:T(1,128)S(1)}, f32[1,3]{1,0:T(1,128)}, u32[]{:S(2)}) copy-start(f32[1,3]{1,0:T(1,128)} %constant.323.clone.1) | copy-start | bytes 40
  63.2 34.1 %copy-start.3 = (f32[32,3,256]{2,0,1:T(8,128)S(1)}, f32[32,3,256]{2,0,1:T(8,128)}, u32[]{:S(2)}) copy-start(f32[32,3,256]{2,0,1:T(8,128)} %param.32) | copy-start | bytes 294916
  63.2 34.1 %copy-start.8 = (s32[32]{0:T(128)S(1)}, s32[32]{0:T(128)}, u32[]{:S(2)}) copy-start(s32[32]{0:T(128)} %param.30) | copy-start | bytes 388
  64.8 33.5 %all-to-all-start = ((f32[59,32,128]{2,0,1:T(8,128)}), f32[59,32,128]{2,0,1:T(8,128)S(1)}, u32[]{:S(2)}, u32[]{:S(2)}) async-start(f32[59,32,128]{2,0,1:T(8,128)} %copy.60), calls=%async_computation | async-start | bytes 2097152 | tf_op jit(solution)/shard_map/all_to_all | solution.py:381
  92.2 18.3 %copy-start.1 = (s32[32,128]{1,0:T(8,128)S(1)}, s32[32,128]{1,0:T(8,128)}, u32[]{:S(2)}) copy-start(s32[32,128]{1,0:T(8,128)} %param.28) | copy-start | bytes 49156
  225.4 6.7 %copy-start.4 = (s32[1,4096]{1,0:T(1,128)S(1)}, s32[1,4096]{1,0:T(1,128)}, u32[]{:S(2)}) copy-start(s32[1,4096]{1,0:T(1,128)} %param.26) | copy-start | bytes 49156
  226.9 31.4 %all-to-all-start.1 = ((f32[59,32,128]{2,0,1:T(8,128)}), f32[59,32,128]{2,0,1:T(8,128)S(1)}, u32[]{:S(2)}, u32[]{:S(2)}) async-start(f32[59,32,128]{2,0,1:T(8,128)} %copy.66), calls=%async_computation.1 | async-start | bytes 2097152 | tf_op jit(solution)/shard_map/all_to_all | solution.py:384
  259.1 86.2 %copy-start = (f32[59,8192]{1,0:T(8,128)S(1)}, f32[59,8192]{1,0:T(8,128)}, u32[]{:S(2)}) copy-start(f32[59,8192]{1,0:T(8,128)} %get-tuple-element.1090) | copy-start | bytes 5799940
  259.1 86.2 %copy-start.7 = (f32[59]{0:T(128)S(1)}, f32[59]{0:T(128)}, u32[]{:S(2)}) copy-start(f32[59]{0:T(128)} %constant.528) | copy-start | bytes 712
  413.3 29.9 %copy-start.9 = (s32[32]{0:T(128)S(1)}, s32[32]{0:T(128)}, u32[]{:S(2)}) copy-start(s32[32]{0:T(128)} %param.31) | copy-start | bytes 388
  414.8 30.0 %all-to-all-start.2 = ((f32[59,32,128]{2,0,1:T(8,128)}), f32[59,32,128]{2,0,1:T(8,128)S(1)}, u32[]{:S(2)}, u32[]{:S(2)}) async-start(f32[59,32,128]{2,0,1:T(8,128)} %copy.70), calls=%async_computation.2 | async-start | bytes 2097152 | tf_op jit(solution)/shard_map/all_to_all | solution.py:396
  418.7 38.7 %copy-start.2 = (s32[32,128]{1,0:T(8,128)S(1)}, s32[32,128]{1,0:T(8,128)}, u32[]{:S(2)}) copy-start(s32[32,128]{1,0:T(8,128)} %param.29) | copy-start | bytes 49156
where the time goes:
time: 503 us; the launch traced here: 494 us
  matrix products  332 us (66%)
  other arithmetic  53.5 us (11%)
  between operations  48.2 us (10%)
  waiting for transfers between devices  28.5 us (6%)
  starting transfers between devices  16.3 us (3%)
  local copies, waits for them, and re-layouts  13.9 us (3%)
    dot_general x16, matrix products, pick_one_block(): jnp.dot(source, selector(source.shape[1], block_ids, source.dtype), preci...  121 us
    dot_general x8, matrix products, return_one_block(): lax.dot_general(block_values, choose, (((1,), (1,)), ((), ())), precision...  85.1 us
    dot_general x8, matrix products, block_inputs(): jnp.dot(buffer, choose, precision=lax.Precision.HIGHEST)  41.3 us
    dot_general x4, matrix products, train_one_block(): lax.dot_general(splat_grad, choose, (((1,), (1,)), ((), ())), precision=l...  29.6 us
    dot_general x12, matrix products, composite(): jnp.einsum('bpj,ji->bpi', log_clear, triangle, precision=lax.Precision.HI...  29.2 us
    all_to_all x1, waiting for transfers between devices, shards(): lax.all_to_all(pullback(splat_grads)[0], 'dev', split_axis=1, concat_axis...  26.1 us
    dot_general x16, matrix products, composite(): jnp.einsum('bpi,cbi->bcp', weight, gathered[6:9], precision=lax.Precision...  24.5 us
    mul x2, other arithmetic, project(): -focal_length * viewed[1] * inverse_depth * inverse_depth  15.2 us
  transfers between devices with their start and end apart: 3, of which 3 were waited for; matrix products, arithmetic and copies ran while one was open for 1% of the time, Pallas kernels for 0%

commit v1 on v0

v1 whole, which is shorter than its diff:
```python
import functools

import jax
import jax.numpy as jnp
import numpy as np
from jax import lax
from jax.experimental import pallas as pl
from jax.experimental.pallas import tpu as pltpu
from jax.sharding import PartitionSpec as P

PARAMS = 59
LIST_LEN = 128
TILE_PIXELS = 256
TILES_X = 128
LANES = 128
ROWS = 9
STRIDE = 72

tile_edge = 16
focal_length = 1000.0
blur_floor = 0.3
adam_epsilon = 1e-08
bias_first = 1.0 - 0.9**20
bias_second = 1.0 - 0.999**20
sh_first = 0.28209479177387814
sh_second = 0.4886025119029199
sh_third = (
    1.0925484305920792,
    -1.0925484305920792,
    0.31539156525252005,
    -1.0925484305920792,
    0.5462742152960396,
)
sh_fourth = (
    -0.5900435899266435,
    2.890611442640554,
    -0.4570457994644658,
    0.3731763325901154,
    -0.4570457994644658,
    1.445305721320277,
    -0.5900435899266435,
)

f32 = jnp.float32
bf16 = jnp.bfloat16
VMEM = pl.BlockSpec(memory_space=pltpu.VMEM)
SMEM = pl.BlockSpec(memory_space=pltpu.SMEM)
ANY = pl.BlockSpec(memory_space=pl.ANY)


def rate_values():
    values = np.full((64,), 0.000125)
    values[0:3] = 0.00016
    values[3:6] = 0.005
    values[6:10] = 0.001
    values[10] = 0.05
    values[11] = 0.0025
    values[27] = 0.0025
    values[43] = 0.0025
    return values


def camera_frame(camera_ref, view):
    shape = (8, LANES)
    angle = [jnp.full(shape, camera_ref[view, k], f32) for k in range(3)]
    shift = [jnp.full(shape, camera_ref[view, 3 + k], f32) for k in range(3)]
    (ca, cb, cc) = [jnp.cos(x) for x in angle]
    (sa, sb, sc) = [jnp.sin(x) for x in angle]
    rot = [
        [cc * cb, cc * sb * sa - sc * ca, cc * sb * ca + sc * sa],
        [sc * cb, sc * sb * sa + cc * ca, sc * sb * ca - cc * sa],
        [-sb, cb * sa, cb * ca],
    ]
    back = [
        rot[0][k] * shift[0] + rot[1][k] * shift[1] + rot[2][k] * shift[2]
        for k in range(3)
    ]
    return rot, shift, back


def sh_terms(x, y, z):
    xx, yy, zz = (x * x, y * y, z * z)
    return [
        -sh_second * y,
        sh_second * z,
        -sh_second * x,
        sh_third[0] * x * y,
        sh_third[1] * y * z,
        sh_third[2] * (2.0 * zz - xx - yy),
        sh_third[3] * x * z,
        sh_third[4] * (xx - yy),
        sh_fourth[0] * y * (3.0 * xx - yy),
        sh_fourth[1] * x * y * z,
        sh_fourth[2] * y * (4.0 * zz - xx - yy),
        sh_fourth[3] * z * (2.0 * zz - 3.0 * xx - 3.0 * yy),
        sh_fourth[4] * x * (4.0 * zz - xx - yy),
        sh_fourth[5] * z * (xx - yy),
        sh_fourth[6] * x * (xx - 3.0 * yy),
    ]


def project(params, frame, half_width, half_height):
    rot, shift, back = frame
    centres = params[0:3]
    viewed = [
        rot[k][0] * centres[0] + rot[k][1] * centres[1] + rot[k][2] * centres[2] + shift[k]
        for k in range(3)
    ]
    inverse = 1.0 / viewed[2]
    scale_z = focal_length * inverse
    u_off = scale_z * viewed[0]
    w_off = scale_z * viewed[1]
    slope_u = u_off * inverse
    slope_w = w_off * inverse
    scales = [jnp.exp(params[3 + k]) for k in range(3)]
    q = params[6:10]
    norm = lax.rsqrt(q[0] * q[0] + q[1] * q[1] + q[2] * q[2] + q[3] * q[3])
    qw, qx, qy, qz = [v * norm for v in q]
    turn = [
        [
            1.0 - 2.0 * (qy * qy + qz * qz),
            2.0 * (qx * qy - qw * qz),
            2.0 * (qx * qz + qw * qy),
        ],
        [
            2.0 * (qx * qy + qw * qz),
            1.0 - 2.0 * (qx * qx + qz * qz),
            2.0 * (qy * qz - qw * qx),
        ],
        [
            2.0 * (qx * qz - qw * qy),
            2.0 * (qy * qz + qw * qx),
            1.0 - 2.0 * (qx * qx + qy * qy),
        ],
    ]
    mapping = [
        [scale_z * rot[0][k] - slope_u * rot[2][k] for k in range(3)],
        [scale_z * rot[1][k] - slope_w * rot[2][k] for k in range(3)],
    ]
    factor = [
        [
            (row[0] * turn[0][k] + row[1] * turn[1][k] + row[2] * turn[2][k]) * scales[k]
            for k in range(3)
        ]
        for row in mapping
    ]
    first, second = factor
    cover_a = first[0] * first[0] + first[1] * first[1] + first[2] * first[2] + blur_floor
    cover_b = first[0] * second[0] + first[1] * second[1] + first[2] * second[2]
    cover_c = second[0] * second[0] + second[1] * second[1] + second[2] * second[2] + blur_floor
    scale_det = 1.0 / (cover_a * cover_c - cover_b * cover_b)
    opacity = 1.0 / (1.0 + jnp.exp(-params[10]))
    towards = [centres[k] + back[k] for k in range(3)]
    length = lax.rsqrt(
        towards[0] * towards[0] + towards[1] * towards[1] + towards[2] * towards[2]
    )
    harmonics = sh_terms(*[v * length for v in towards])
    colours = []
    for channel in range(3):
        running = 0.5 + sh_first * params[11 + 16 * channel]
        for term in range(15):
            running = running + harmonics[term] * params[12 + 16 * channel + term]
        colours.append(jnp.maximum(running, 0.0))
    return [
        u_off + half_width,
        w_off + half_height,
        cover_c * scale_det,
        -cover_b * scale_det,
        cover_a * scale_det,
        opacity,
    ] + colours


def permute(idx_ref, main_ref, last_ref, chunks, rows, write):
    def group_step(group, unused):
        base = pl.multiple_of(group * 8, 8)
        index = idx_ref[pl.ds(base, 8), :]
        high = index >> 7
        low = index & 127
        highs = [jnp.broadcast_to(high[k : k + 1], (8, LANES)) for k in range(8)]
        lows = [jnp.broadcast_to(low[k : k + 1], (8, LANES)) for k in range(8)]
        totals = [jnp.zeros((8, LANES), f32) for k in range(9)]
        for chunk in range(chunks):
            source = main_ref[chunk]
            for k in range(8):
                found = jnp.take_along_axis(
                    source, lows[k], axis=1, mode="promise_in_bounds"
                )
                totals[k] = jnp.where(highs[k] == chunk, found, totals[k])
            source = jnp.broadcast_to(last_ref[chunk : chunk + 1, :], (8, LANES))
            found = jnp.take_along_axis(source, low, axis=1, mode="promise_in_bounds")
            totals[8] = jnp.where(high == chunk, found, totals[8])
        write(group, totals[:8], totals[8])
        return unused

    lax.fori_loop(0, rows // 8, group_step, 0)


def invert(idx_ref, rows, high_count, inverse_ref):
    index = idx_ref[...]
    high = index >> 7
    low = index & 127
    high_ids = lax.broadcasted_iota(jnp.int32, (high_count, LANES), 0)
    low_ids = lax.broadcasted_iota(jnp.int32, (LANES, LANES), 0)
    lane_ids = lax.broadcasted_iota(jnp.int32, (high_count, LANES), 1).astype(f32)
    total = jnp.zeros((2 * high_count, LANES), f32)
    for start in range(0, rows, 8):
        left = []
        right = []
        for row in range(start, start + 8):
            here = high[row : row + 1] == high_ids
            left.append(
                jnp.concatenate(
                    [jnp.where(here, row + 1.0, 0.0), jnp.where(here, lane_ids, 0.0)], axis=0
                ).astype(bf16)
            )
            right.append(jnp.where(low[row : row + 1] == low_ids, 1.0, 0.0).astype(bf16))
        total = total + lax.dot_general(
            jnp.concatenate(left, axis=1),
            jnp.concatenate(right, axis=1),
            (((1,), (1,)), ((), ())),
            preferred_element_type=f32,
        )
    rows_found = total[:high_count].astype(jnp.int32)
    lanes_found = total[high_count:].astype(jnp.int32)
    inverse_ref[...] = (rows_found - 1) * LANES + lanes_found


def unpack(packed_ref, main_ref, last_ref, chunks):
    for chunk in range(chunks):
        for k in range(8):
            main_ref[chunk, k : k + 1, :] = packed_ref[chunk, :, k * LANES : (k + 1) * LANES]
        last_ref[chunk : chunk + 1, :] = packed_ref[chunk, :, 8 * LANES : 9 * LANES]


def pack_group(packed_ref):
    def write(group, vectors, last):
        for k in range(8):
            row = group * 8 + k
            for item in range(8):
                packed_ref[row, :, item * LANES : (item + 1) * LANES] = vectors[k][
                    item : item + 1
                ]
            packed_ref[row, :, 8 * LANES : 9 * LANES] = last[k : k + 1]

    return write


def slots_as_rows(slots_ref, idx_ref, rows):
    for row in range(rows):
        idx_ref[row : row + 1, :] = slots_ref[:, row * LANES : (row + 1) * LANES]


def to_dense(native, dense_ref, row_block, chunk):
    if native.shape[0] == 8:
        dense_ref[pl.ds(8 * row_block * STRIDE + chunk, 8, stride=STRIDE), :] = native
    else:
        for k in range(native.shape[0]):
            dense_ref[pl.ds((8 * row_block + k) * STRIDE + chunk, 1), :] = native[k : k + 1]


def dense_load(dense_ref, row, group):
    return dense_ref[pl.ds(pl.multiple_of(row * STRIDE + group * 8, 8), 8), :]


def dense_store(dense_ref, row, group, value):
    dense_ref[pl.ds(pl.multiple_of(row * STRIDE + group * 8, 8), 8), :] = value


def row_blocks():
    return [(block, min(8, PARAMS - 8 * block)) for block in range((PARAMS + 7) // 8)]


def project_groups(dense_ref, splat_ref, frame, half_width, half_height, chunks):
    def step(group, unused):
        params = [dense_load(dense_ref, row, group) for row in range(PARAMS)]
        for row, value in enumerate(project(params, frame, half_width, half_height)):
            dense_store(splat_ref, row, group, value)
        return unused

    lax.fori_loop(0, chunks // 8, step, 0)


def send_splats(splat_ref, main_ref, idx_ref, packed_ref, chunks, rows):
    for chunk in range(chunks):
        main_ref[chunk] = splat_ref[pl.ds(chunk, 8, stride=STRIDE), :]
    last_ref = splat_ref.at[pl.ds(8 * STRIDE, chunks), :]
    permute(idx_ref, main_ref, last_ref, chunks, rows, pack_group(packed_ref))


def first_owner_body(
    half_width,
    half_height,
    camera_ref,
    params_ref,
    slots_ref,
    packed_ref,
    dense_ref,
    splat_ref,
    main_ref,
    idx_ref,
):
    chunks = params_ref.shape[1] // LANES
    rows = slots_ref.shape[1] // LANES
    slots_as_rows(slots_ref, idx_ref, rows)

    def relayout(chunk, unused):
        lanes = pl.ds(pl.multiple_of(chunk * LANES, LANES), LANES)
        for block, size in row_blocks():
            to_dense(params_ref[8 * block : 8 * block + size, lanes], dense_ref, block, chunk)
        return unused

    lax.fori_loop(0, chunks, relayout, 0, unroll=4)
    frame = camera_frame(camera_ref, 0)
    project_groups(dense_ref, splat_ref, frame, half_width, half_height, chunks)
    send_splats(splat_ref, main_ref, idx_ref, packed_ref, chunks, rows)


def first_owner(camera, params, slots, half_width, half_height):
    chunks = params.shape[1] // LANES
    rows = slots.shape[1] // LANES
    return pl.pallas_call(
        functools.partial(first_owner_body, half_width, half_height),
        out_shape=jax.ShapeDtypeStruct((rows, 1, ROWS * LANES), f32),
        in_specs=[SMEM, VMEM, VMEM],
        out_specs=VMEM,
        scratch_shapes=[
            pltpu.VMEM((64 * STRIDE, LANES), f32),
            pltpu.VMEM((ROWS * STRIDE, LANES), f32),
            pltpu.VMEM((chunks, 8, LANES), f32),
            pltpu.VMEM((rows, LANES), jnp.int32),
        ],
        name="first_owner",
    )(camera, params, slots)


def second_owner_body(
    half_width,
    half_height,
    camera_ref,
    params_ref,
    first_hbm,
    second_hbm,
    slots_ref,
    next_slots_ref,
    packed_ref,
    out_params_hbm,
    out_first_hbm,
    out_second_hbm,
    out_packed_ref,
    dense_ref,
    grad_ref,
    splat_ref,
    main_ref,
    last_ref,
    idx_ref,
    inverse_ref,
    params_out_ref,
    first_ref,
    second_ref,
    load_sems,
    store_sems,
):
    chunks = params_ref.shape[1] // LANES
    rows = slots_ref.shape[1] // LANES
    loads = [
        pltpu.make_async_copy(first_hbm, first_ref, load_sems.at[0]),
        pltpu.make_async_copy(second_hbm, second_ref, load_sems.at[1]),
    ]
    for copy in loads:
        copy.start()
    slots_as_rows(slots_ref, idx_ref, rows)
    invert(idx_ref, rows, chunks, inverse_ref)
    unpack(packed_ref, main_ref, last_ref, rows)

    def relayout(chunk, unused):
        lanes = pl.ds(pl.multiple_of(chunk * LANES, LANES), LANES)
        for block, size in row_blocks():
            to_dense(params_ref[8 * block : 8 * block + size, lanes], dense_ref, block, chunk)
        return unused

    lax.fori_loop(0, chunks, relayout, 0, unroll=4)

    def write_columns(group, vectors, last):
        for k in range(8):
            splat_ref[pl.ds(group * 8 + k, 8, stride=STRIDE), :] = vectors[k]
        dense_store(splat_ref, 8, group, last)

    permute(inverse_ref, main_ref, last_ref, rows, chunks, write_columns)

    frame = camera_frame(camera_ref, 0)

    def pull_step(group, unused):
        params = [dense_load(dense_ref, row, group) for row in range(PARAMS)]
        splats, pullback = jax.vjp(
            lambda *p: project(list(p), frame, half_width, half_height), *params
        )
        cotangents = [dense_load(splat_ref, row, group) for row in range(ROWS)]
        through_opacity = cotangents[5] * (1.0 - splats[5])
        cotangents[5] = jnp.zeros_like(cotangents[5])
        grads = list(pullback(cotangents))
        grads[10] = through_opacity
        for row, value in enumerate(grads):
            dense_store(grad_ref, row, group, value)
        return unused

    lax.fori_loop(0, chunks // 8, pull_step, 0)

    for copy in loads:
        copy.wait()
    rates = rate_values() / bias_first
    stores = []
    row_ids = lax.broadcasted_iota(jnp.int32, (8, LANES), 0)
    for block, size in row_blocks():
        span = slice(8 * block, 8 * block + size)
        block_rates = rates[8 * block : 8 * block + 8]
        step_size = jnp.full((8, LANES), block_rates[0], f32)
        for k in range(1, 8):
            if block_rates[k] != block_rates[0]:
                step_size = jnp.where(row_ids == k, f32(block_rates[k]), step_size)
        step_size = step_size[:size]

        def adam_step(chunk, unused, block=block, size=size, span=span, step_size=step_size):
            lanes = pl.ds(pl.multiple_of(chunk * LANES, LANES), LANES)
            gradient = grad_ref[pl.ds(8 * block * STRIDE + chunk, 8, stride=STRIDE), :][:size]
            moment = 0.9 * first_ref[span, lanes] + 0.1 * gradient
            square = 0.999 * second_ref[span, lanes] + 0.001 * gradient * gradient
            scaled = square * (1.0 / bias_second)
            root = scaled * lax.rsqrt(scaled)
            fresh = params_ref[span, lanes] - step_size * moment / (root + adam_epsilon)
            first_ref[span, lanes] = moment
            second_ref[span, lanes] = square
            params_out_ref[span, lanes] = fresh
            to_dense(fresh, dense_ref, block, chunk)
            return unused

        lax.fori_loop(0, chunks, adam_step, 0, unroll=8)
        for number, (source, target) in enumerate(
            [
                (params_out_ref, out_params_hbm),
                (first_ref, out_first_hbm),
                (second_ref, out_second_hbm),
            ]
        ):
            copy = pltpu.make_async_copy(
                source.at[span, :], target.at[span, :], store_sems.at[number, block]
            )
            copy.start()
            stores.append(copy)

    slots_as_rows(next_slots_ref, idx_ref, rows)
    frame = camera_frame(camera_ref, 1)
    project_groups(dense_ref, splat_ref, frame, half_width, half_height, chunks)
    send_splats(splat_ref, main_ref, idx_ref, out_packed_ref, chunks, rows)
    for copy in stores:
        copy.wait()


def second_owner(camera, params, first, second, slots, next_slots, packed, half_width, half_height):
    chunks = params.shape[1] // LANES
    rows = slots.shape[1] // LANES
    shape = jax.ShapeDtypeStruct(params.shape, f32)
    return pl.pallas_call(
        functools.partial(second_owner_body, half_width, half_height),
        out_shape=(shape, shape, shape, jax.ShapeDtypeStruct((rows, 1, ROWS * LANES), f32)),
        in_specs=[SMEM, VMEM, ANY, ANY, VMEM, VMEM, VMEM],
        out_specs=(ANY, ANY, ANY, VMEM),
        scratch_shapes=[
            pltpu.VMEM((64 * STRIDE, LANES), f32),
            pltpu.VMEM((64 * STRIDE, LANES), f32),
            pltpu.VMEM((ROWS * STRIDE, LANES), f32),
            pltpu.VMEM((max(chunks, rows), 8, LANES), f32),
            pltpu.VMEM((rows, LANES), f32),
            pltpu.VMEM((rows, LANES), jnp.int32),
            pltpu.VMEM((chunks, LANES), jnp.int32),
            pltpu.VMEM(params.shape, f32),
            pltpu.VMEM(params.shape, f32),
            pltpu.VMEM(params.shape, f32),
            pltpu.SemaphoreType.DMA((2,)),
            pltpu.SemaphoreType.DMA((3, 8)),
        ],
        name="second_owner",
    )(camera, params, first, second, slots, next_slots, packed)


def halves(value):
    high = value.astype(bf16)
    return high, (value - high.astype(f32)).astype(bf16)


def triangle_pair(forward):
    rows = lax.broadcasted_iota(jnp.int32, (LIST_LEN, LIST_LEN), 0)
    cols = lax.broadcasted_iota(jnp.int32, (LIST_LEN, LIST_LEN), 1)
    chosen = rows < cols if forward else rows > cols
    one = jnp.where(chosen, 1.0, 0.0).astype(bf16)
    return jnp.concatenate([one, one], axis=0)


def batch_tiles(tile_count):
    return 8 if tile_count % 8 == 0 else 1


def tile_offsets(splat_ref, tile, number):
    left = (number % TILES_X) * tile_edge
    top = (number // TILES_X) * tile_edge
    ids = lax.broadcasted_iota(jnp.int32, (8, LANES), 0)
    u = jnp.broadcast_to(splat_ref[tile, 0:1, :], (8, LANES))
    w = jnp.broadcast_to(splat_ref[tile, 1:2, :], (8, LANES))
    across = [u - ((ids + (left + 8 * h)).astype(f32) + 0.5) for h in range(2)]
    down = [w - ((ids + (top + 8 * h)).astype(f32) + 0.5) for h in range(2)]
    return across, down


def spread_row(ref, row):
    return jnp.broadcast_to(ref[row : row + 1, :], (8, LANES))


def alpha_phase(splat_ref, tile, number, base, row_ref, alpha_ref, odds_ref, pair_ref):
    a, b, c, o = [jnp.broadcast_to(splat_ref[tile, k : k + 1, :], (8, LANES)) for k in (2, 3, 4, 5)]
    across, down = tile_offsets(splat_ref, tile, number)
    along = [(-0.5 * a) * x * x for x in across]
    for h in range(2):
        row_ref[8 * h : 8 * h + 8, :] = (-0.5 * c) * down[h] * down[h]
        row_ref[16 + 8 * h : 24 + 8 * h, :] = -(b * down[h])
    for row in range(tile_edge):
        fixed = spread_row(row_ref, row)
        slope = spread_row(row_ref, 16 + row)
        logs = []
        for h in range(2):
            exponent = along[h] + (fixed + slope * across[h])
            alpha = o * jnp.exp(exponent)
            log_clear = jnp.log(1.0 - alpha)
            where = pl.ds(base + row * tile_edge + 8 * h, 8)
            alpha_ref[where, :] = alpha
            if odds_ref is not None:
                odds_ref[where, :] = alpha * jnp.exp(-log_clear)
            logs.append(log_clear)
        high, low = halves(jnp.concatenate(logs, axis=0))
        where = pl.ds(base + row * tile_edge, tile_edge)
        pair_ref[where, :LIST_LEN] = high
        pair_ref[where, LIST_LEN:] = low


def weight_phase(base, before_ref, alpha_ref, weight_ref, pair_ref):
    for row in range(tile_edge):
        where = pl.ds(base + row * tile_edge, tile_edge)
        weight = alpha_ref[where, :] * jnp.exp(before_ref[where, :])
        if weight_ref is not None:
            weight_ref[where, :] = weight
        high, low = halves(weight)
        pair_ref[where, :LIST_LEN] = high
        pair_ref[where, LIST_LEN:] = low


def split_colours(splat_ref, tile):
    colours = splat_ref[tile, 6:14, :]
    high = colours.astype(bf16).astype(f32)
    return high, colours - high


def colour_sum(high, low, pair):
    upper = jnp.concatenate([high, high], axis=1)
    lower = jnp.concatenate([low, jnp.zeros_like(low)], axis=1)
    result = lax.dot_general(
        jnp.concatenate([upper, lower], axis=0).astype(bf16),
        pair,
        (((1,), (1,)), ((), ())),
        preferred_element_type=f32,
    )
    return result[0:8] + result[8:16]


def gather_tiles(lists_ref, packed_ref, main_ref, last_ref, splat_ref):
    chunks = packed_ref.shape[0]
    tile_count = lists_ref.shape[0]
    unpack(packed_ref, main_ref, last_ref, chunks)

    def write(group, vectors, last):
        for k in range(8):
            tile = group * 8 + k
            splat_ref[tile, 0:8, :] = vectors[k]
            splat_ref[tile, 8:9, :] = last[k : k + 1]
            splat_ref[tile, 9:16, :] = jnp.zeros((7, LANES), f32)

    permute(lists_ref, main_ref, last_ref, chunks, tile_count, write)


def train_body(
    numbers_ref,
    lists_ref,
    targets_ref,
    packed_ref,
    out_packed_ref,
    main_ref,
    last_ref,
    splat_ref,
    row_ref,
    alpha_ref,
    odds_ref,
    plain_ref,
    weight_ref,
    pair_ref,
    grad_pair_ref,
    grad_ref,
    grad_last_ref,
    inverse_ref,
):
    tile_count = lists_ref.shape[0]
    batch = batch_tiles(tile_count)
    gather_tiles(lists_ref, packed_ref, main_ref, last_ref, splat_ref)
    invert(lists_ref, tile_count, packed_ref.shape[0], inverse_ref)
    forward = triangle_pair(True)
    backward = triangle_pair(False)

    def batch_step(step, unused):
        first = step * batch

        def alphas(k, unused):
            tile = first + k
            base = pl.multiple_of(k * TILE_PIXELS, TILE_PIXELS)
            alpha_phase(
                splat_ref, tile, numbers_ref[tile], base, row_ref, alpha_ref, odds_ref, pair_ref
            )
            return unused

        lax.fori_loop(0, batch, alphas, 0)
        plain_ref[...] = jnp.dot(pair_ref[...], forward, preferred_element_type=f32)

        def weights(k, unused):
            base = pl.multiple_of(k * TILE_PIXELS, TILE_PIXELS)
            weight_phase(base, plain_ref, alpha_ref, weight_ref, pair_ref)
            return unused

        lax.fori_loop(0, batch, weights, 0)

        for k in range(batch):
            tile = first + k
            span = slice(k * TILE_PIXELS, (k + 1) * TILE_PIXELS)
            pair = pair_ref[span, :]
            high, low = split_colours(splat_ref, tile)
            rendered = colour_sum(high, low, pair)
            wanted = targets_ref[tile]
            wanted = jnp.concatenate([wanted, jnp.zeros((5, TILE_PIXELS), f32)], axis=0)
            delta = rendered - wanted
            delta_high = delta.astype(bf16).astype(f32)
            delta_low = delta - delta_high
            left = jnp.concatenate(
                [delta_high, delta_high, delta_low, jnp.zeros_like(delta)], axis=0
            ).astype(bf16)
            right = jnp.concatenate([high, low, high, jnp.zeros_like(high)], axis=0).astype(bf16)
            plain_ref[span, :] = lax.dot_general(
                left, right, (((0,), (0,)), ((), ())), preferred_element_type=f32
            )
            colour = jnp.dot(
                jnp.concatenate([delta_high, delta_low], axis=0).astype(bf16),
                pair,
                preferred_element_type=f32,
            )
            colour = colour[0:8, :LIST_LEN] + (colour[0:8, LIST_LEN:] + colour[8:16, :LIST_LEN])
            grad_ref[tile, 6:8, :] = colour[0:2]
            grad_last_ref[pl.ds(tile, 1), :] = colour[2:3]

        def pulls(k, unused):
            for row in range(tile_edge):
                where = pl.ds(pl.multiple_of(k * TILE_PIXELS, TILE_PIXELS) + row * tile_edge, tile_edge)
                product = plain_ref[where, :] * weight_ref[where, :]
                weight_ref[where, :] = product
                high, low = halves(product)
                grad_pair_ref[where, :LIST_LEN] = high
                grad_pair_ref[where, LIST_LEN:] = low
            return unused

        lax.fori_loop(0, batch, pulls, 0)
        plain_ref[...] = jnp.dot(grad_pair_ref[...], backward, preferred_element_type=f32)

        def moments(k, unused):
            tile = first + k
            base = pl.multiple_of(k * TILE_PIXELS, TILE_PIXELS)
            across, down = tile_offsets(splat_ref, tile, numbers_ref[tile])
            for h in range(2):
                row_ref[8 * h : 8 * h + 8, :] = down[h]
            sums = [[jnp.zeros((8, LANES), f32) for j in range(3)] for h in range(2)]
            for row in range(tile_edge):
                offset = spread_row(row_ref, row)
                for h in range(2):
                    where = pl.ds(base + row * tile_edge + 8 * h, 8)
                    slope = weight_ref[where, :] - plain_ref[where, :] * odds_ref[where, :]
                    once = slope * offset
                    sums[h][0] = sums[h][0] + slope
                    sums[h][1] = sums[h][1] + once
                    sums[h][2] = sums[h][2] + once * offset

            def total(parts):
                return jnp.sum(parts[0] + parts[1], axis=0, keepdims=True)

            whole = total([sums[h][0] for h in range(2)])
            along = [sums[h][0] * across[h] for h in range(2)]
            moment_x = total(along)
            moment_xx = total([along[h] * across[h] for h in range(2)])
            moment_y = total([sums[h][1] for h in range(2)])
            moment_xy = total([sums[h][1] * across[h] for h in range(2)])
            moment_yy = total([sums[h][2] for h in range(2)])
            a = splat_ref[tile, 2:3, :]
            b = splat_ref[tile, 3:4, :]
            c = splat_ref[tile, 4:5, :]
            grad_ref[tile, 0:1, :] = -(a * moment_x + b * moment_y)
            grad_ref[tile, 1:2, :] = -(c * moment_y + b * moment_x)
            grad_ref[tile, 2:3, :] = -0.5 * moment_xx
            grad_ref[tile, 3:4, :] = -moment_xy
            grad_ref[tile, 4:5, :] = -0.5 * moment_yy
            grad_ref[tile, 5:6, :] = whole
            return unused

        lax.fori_loop(0, batch, moments, 0)
        return unused

    lax.fori_loop(0, tile_count // batch, batch_step, 0)
    permute(
        inverse_ref,
        grad_ref,
        grad_last_ref,
        tile_count,
        out_packed_ref.shape[0],
        pack_group(out_packed_ref),
    )


def train(numbers, lists, targets, packed):
    tile_count = lists.shape[0]
    chunks = packed.shape[0]
    pixels = batch_tiles(tile_count) * TILE_PIXELS
    return pl.pallas_call(
        train_body,
        out_shape=jax.ShapeDtypeStruct(packed.shape, f32),
        in_specs=[SMEM, VMEM, VMEM, VMEM],
        out_specs=VMEM,
        scratch_shapes=[
            pltpu.VMEM((chunks, 8, LANES), f32),
            pltpu.VMEM((chunks, LANES), f32),
            pltpu.VMEM((tile_count, 16, LANES), f32),
            pltpu.VMEM((32, LANES), f32),
            pltpu.VMEM((pixels, LIST_LEN), f32),
            pltpu.VMEM((pixels, LIST_LEN), f32),
            pltpu.VMEM((pixels, LIST_LEN), f32),
            pltpu.VMEM((pixels, LIST_LEN), f32),
            pltpu.VMEM((pixels, 2 * LIST_LEN), bf16),
            pltpu.VMEM((pixels, 2 * LIST_LEN), bf16),
            pltpu.VMEM((tile_count, 8, LANES), f32),
            pltpu.VMEM((tile_count, LANES), f32),
            pltpu.VMEM((chunks, LANES), jnp.int32),
        ],
        name="train_tiles",
    )(numbers, lists, targets, packed)


def render_body(
    numbers_ref,
    lists_ref,
    packed_ref,
    out_ref,
    main_ref,
    last_ref,
    splat_ref,
    row_ref,
    alpha_ref,
    plain_ref,
    pair_ref,
):
    tile_count = lists_ref.shape[0]
    batch = batch_tiles(tile_count)
    gather_tiles(lists_ref, packed_ref, main_ref, last_ref, splat_ref)
    forward = triangle_pair(True)

    def batch_step(step, unused):
        first = step * batch

        def alphas(k, unused):
            tile = first + k
            base = pl.multiple_of(k * TILE_PIXELS, TILE_PIXELS)
            alpha_phase(splat_ref, tile, numbers_ref[tile], base, row_ref, alpha_ref, None, pair_ref)
            return unused

        lax.fori_loop(0, batch, alphas, 0)
        plain_ref[...] = jnp.dot(pair_ref[...], forward, preferred_element_type=f32)

        def weights(k, unused):
            base = pl.multiple_of(k * TILE_PIXELS, TILE_PIXELS)
            weight_phase(base, plain_ref, alpha_ref, None, pair_ref)
            return unused

        lax.fori_loop(0, batch, weights, 0)
        for k in range(batch):
            tile = first + k
            high, low = split_colours(splat_ref, tile)
            pair = pair_ref[k * TILE_PIXELS : (k + 1) * TILE_PIXELS, :]
            out_ref[tile] = colour_sum(high, low, pair)[0:3]
        return unused

    lax.fori_loop(0, tile_count // batch, batch_step, 0)


def render(numbers, lists, packed):
    tile_count = lists.shape[0]
    chunks = packed.shape[0]
    pixels = batch_tiles(tile_count) * TILE_PIXELS
    return pl.pallas_call(
        render_body,
        out_shape=jax.ShapeDtypeStruct((tile_count, 3, TILE_PIXELS), f32),
        in_specs=[SMEM, VMEM, VMEM],
        out_specs=VMEM,
        scratch_shapes=[
            pltpu.VMEM((chunks, 8, LANES), f32),
            pltpu.VMEM((chunks, LANES), f32),
            pltpu.VMEM((tile_count, 16, LANES), f32),
            pltpu.VMEM((32, LANES), f32),
            pltpu.VMEM((pixels, LIST_LEN), f32),
            pltpu.VMEM((pixels, LIST_LEN), f32),
            pltpu.VMEM((pixels, 2 * LIST_LEN), bf16),
        ],
        name="render_tiles",
    )(numbers, lists, packed)


def exchange(packed, devices):
    rows = packed.shape[0]
    if rows == devices:
        return lax.all_to_all(packed, "dev", split_axis=0, concat_axis=0, tiled=True)
    cap = rows * LANES // devices
    slots = packed.reshape(rows, ROWS, LANES).transpose(1, 0, 2).reshape(ROWS, devices, cap)
    slots = lax.all_to_all(slots, "dev", split_axis=1, concat_axis=1, tiled=True)
    slots = slots.reshape(ROWS, rows, LANES).transpose(1, 0, 2)
    return slots.reshape(rows, 1, ROWS * LANES)


def shards(
    gauss_params,
    adam_first,
    adam_second,
    camera,
    send_first,
    send_second,
    lists_first,
    lists_second,
    tiles_first,
    tiles_second,
    targets,
):
    devices = lax.axis_size("dev")
    half_width = 0.5 * TILES_X * tile_edge
    half_height = 0.5 * (lists_first.shape[0] * devices // TILES_X * tile_edge)
    packed = first_owner(camera, gauss_params, send_first, half_width, half_height)
    packed = exchange(packed, devices)
    packed = train(tiles_first, lists_first, targets, packed)
    packed = exchange(packed, devices)
    new_params, new_first, new_second, packed = second_owner(
        camera,
        gauss_params,
        adam_first,
        adam_second,
        send_first,
        send_second,
        packed,
        half_width,
        half_height,
    )
    packed = exchange(packed, devices)
    rendered = render(tiles_second, lists_second, packed)
    return (new_params, new_first, new_second, rendered)


def solution(mesh):
    placed = (
        P(None, "dev"),
        P(None, "dev"),
        P(None, "dev"),
        P(),
        P("dev", None),
        P("dev", None),
        P("dev", None),
        P("dev", None),
        P("dev"),
        P("dev"),
        P("dev", None, None),
    )
    return jax.shard_map(
        shards,
        mesh=mesh,
        in_specs=placed,
        out_specs=(P(None, "dev"), P(None, "dev"), P(None, "dev"), P("dev", None, None)),
        check_vma=False,
    )
```

time: 503 us -> 120 us (0.24); the launches traced: 494 us -> 119 us
  matrix products: 332 us -> 0 us
  Pallas kernels: 0 us -> 77.5 us
  other arithmetic: 53.5 us -> 0 us
  between operations: 48.2 us -> 0.67 us
  blocking collectives: 0 us -> 23.4 us
  waiting for transfers between devices: 28.5 us -> 7.68 us
  local copies, waits for them, and re-layouts: 13.9 us -> 2.95 us
  starting transfers between devices: 16.3 us -> 7.33 us
    dot_general x68 -> x0, matrix products: 332 us -> none  [the longest x16 121 us: pick_one_block(): jnp.dot(source, selector(source.shape[1], block_ids, source.dtype), preci...]
    pallas_call x0 -> x4, Pallas kernels: none -> 77.5 us  [the longest x1 29.6 us: train(): pl.pallas_call(train_body, out_shape=jax.ShapeDtypeStruct(packed.shape, f...]
    mul x45 -> x0, other arithmetic: 30.6 us -> none  [the longest x2 15.2 us: project(): -focal_length * viewed[1] * inverse_depth * inverse_depth]
    all_to_all x0 -> x2, blocking collectives: none -> 23.4 us  [exchange(): lax.all_to_all(packed, 'dev', split_axis=0, concat_axis=0, tiled=True)]
    all_to_all x3 -> x1, waiting for transfers between devices: 28.5 us -> 7.68 us  [exchange(): lax.all_to_all(packed, 'dev', split_axis=0, concat_axis=0, tiled=True)]
    all_to_all x3 -> x1, starting transfers between devices: 16.3 us -> 7.33 us  [exchange(): lax.all_to_all(packed, 'dev', split_axis=0, concat_axis=0, tiled=True)]
    sub x1 -> x0, other arithmetic: 6.35 us -> none  [shards(): gauss_params - step_sizes * (new_first / bias_first) / (jnp.sqrt(new_seco...]
    all_to_all x8 -> x0, local copies, waits for them, and re-layouts: 5.51 us -> none  [the longest x4 2.31 us: shards(): lax.all_to_all(pullback(splat_grads)[0], 'dev', split_axis=1, concat_axis...]
  transfers between devices with their start and end apart: 3 -> 1, of which waited for: 3 -> 1; matrix products, arithmetic and copies ran while one was open for 1% -> 1% of each run, Pallas kernels for 0% -> 0%
where the time goes in v1:
time: 120 us; the launch traced here: 119 us
  Pallas kernels  77.5 us (65%)
  blocking collectives  23.4 us (20%)
  waiting for transfers between devices  7.68 us (6%)
  starting transfers between devices  7.33 us (6%)
  local copies, waits for them, and re-layouts  2.95 us (2%)
    pallas_call x1, Pallas kernels, train(): pl.pallas_call(train_body, out_shape=jax.ShapeDtypeStruct(packed.shape, f...  29.6 us
    all_to_all x2, blocking collectives, exchange(): lax.all_to_all(packed, 'dev', split_axis=0, concat_axis=0, tiled=True)  23.4 us
    pallas_call x1, Pallas kernels, second_owner(): pl.pallas_call(functools.partial(second_owner_body, half_width, half_heig...  23.2 us
    pallas_call x1, Pallas kernels, render(): pl.pallas_call(render_body, out_shape=jax.ShapeDtypeStruct((tile_count, 3...  14.5 us
    pallas_call x1, Pallas kernels, first_owner(): pl.pallas_call(functools.partial(first_owner_body, half_width, half_heigh...  10.1 us
    all_to_all x1, waiting for transfers between devices, exchange(): lax.all_to_all(packed, 'dev', split_axis=0, concat_axis=0, tiled=True)  7.68 us
    all_to_all x1, starting transfers between devices, exchange(): lax.all_to_all(packed, 'dev', split_axis=0, concat_axis=0, tiled=True)  7.33 us
    unnamed x6, local copies, waits for them, and re-layouts  2.95 us
  transfers between devices with their start and end apart: 1, of which 1 were waited for; matrix products, arithmetic and copies ran while one was open for 1% of the time, Pallas kernels for 0%

profile of v1, /device:TPU:0, one launch (start us, length us, event | category | flops | bytes accessed | tf_op | source)
XLA Modules:
  0.0 119.5 jit_solution(9326851408633309324)
XLA Ops:
  0.6 0.0 copy-start.1
  0.6 10.1 %first_owner.1 = f32[32,1,1152]{2,1,0:T(1,128)} custom-call(f32[2,6]{1,0:T(2,128)} %camera_ref.3, f32[59,8192]{1,0:T(8,128)} %params_ref.3, s32[1,4096]{1,0:T(1,128)} %slots_ref.3), custom_call_target="tpu_custom_call" | custom-call | tf_op jit(solution)/shard_map/first_owner/pallas_call | solution.py:322
  10.8 7.3 %all-to-all-start = ((f32[32,1,1152]{2,1,0:T(1,128)}), f32[32,1,1152]{2,1,0:T(1,128)S(1)}, u32[]{:S(2)}, u32[]{:S(2)}) async-start(f32[32,1,1152]{2,1,0:T(1,128)} %first_owner.1), calls=%async_computation | async-start | bytes 294912 | tf_op jit(solution)/shard_map/all_to_all | solution.py:827
  18.1 0.0 copy-done.1
  18.1 0.7 copy.15.targets_ref
  18.8 7.7 %all-to-all-done.packed_ref = f32[32,1,1152]{2,1,0:T(1,128)S(1)} async-done(((f32[32,1,1152]{2,1,0:T(1,128)}), f32[32,1,1152]{2,1,0:T(1,128)S(1)}, u32[]{:S(2)}, u32[]{:S(2)}) %all-to-all-start) | async-done | bytes 147488 | tf_op jit(solution)/shard_map/all_to_all | solution.py:827
  26.5 0.0 copy-start
  26.5 0.7 copy-done
  27.2 29.6 %train_tiles.1 = f32[32,1,1152]{2,1,0:T(1,128)} custom-call(s32[32]{0:T(128)} %numbers_ref.2, s32[32,128]{1,0:T(8,128)} %lists_ref.2, f32[32,3,256]{2,1,0:T(4,128)} %copy.15.targets_ref, f32[32,1,1152]{2,1,0:T(1,128)} %copy-done), custom_call_target="tpu_custom_call" | custom-call | tf_op jit(solution)/shard_map/train_tiles/pallas_call | solution.py:732
  56.7 11.7 %all_to_all.15.packed_ref = f32[32,1,1152]{2,1,0:T(1,128)} all-to-all(f32[32,1,1152]{2,1,0:T(1,128)} %train_tiles.1), channel_id=1, replica_groups=mesh['dev'=32] {'dev'}, dimensions={0} | all-to-all | bytes 294912 | tf_op jit(solution)/shard_map/all_to_all | solution.py:827
  68.4 23.2 %second_owner.1 = (f32[59,8192]{1,0:T(8,128)}, f32[59,8192]{1,0:T(8,128)}, f32[59,8192]{1,0:T(8,128)}, f32[32,1,1152]{2,1,0:T(1,128)}) custom-call(f32[2,6]{1,0:T(2,128)} %camera_ref.3, f32[59,8192]{1,0:T(8,128)} %params_ref.3, f32[59,8192]{1,0:T(8,128)} %first_hbm.1, f32[59,8192]{1,0:T(8,128)} %second_hbm.1, s32[1,4096]{1,0:T(1,128)} %slots_ref.3, ...), custom_call_target="tpu_custom_call" | custom-call | tf_op jit(solution)/shard_map/second_owner/pallas_call | solution.py:463
  91.7 11.7 %all_to_all.16.packed_ref = f32[32,1,1152]{2,1,0:T(1,128)} all-to-all(f32[32,1,1152]{2,1,0:T(1,128)} %get-tuple-element.11), channel_id=1, replica_groups=mesh['dev'=32] {'dev'}, dimensions={0} | all-to-all | bytes 294912 | tf_op jit(solution)/shard_map/all_to_all | solution.py:827
  103.4 14.5 %render_tiles.1 = f32[32,3,256]{2,1,0:T(4,128)} custom-call(s32[32]{0:T(128)} %numbers_ref.3, s32[32,128]{1,0:T(8,128)} %lists_ref.3, f32[32,1,1152]{2,1,0:T(1,128)} %all_to_all.16.packed_ref), custom_call_target="tpu_custom_call" | custom-call | tf_op jit(solution)/shard_map/render_tiles/pallas_call | solution.py:806
  117.9 1.6 %copy.16 = f32[32,3,256]{2,0,1:T(8,128)} copy(f32[32,3,256]{2,1,0:T(4,128)} %render_tiles.1) | data formatting | bytes 196608
Async XLA Ops:
  0.6 17.5 %copy-start.1 = (f32[32,3,256]{2,0,1:T(8,128)S(1)}, f32[32,3,256]{2,0,1:T(8,128)}, u32[]{:S(2)}) copy-start(f32[32,3,256]{2,0,1:T(8,128)} %param.21) | copy-start | bytes 294916
  10.8 15.7 %all-to-all-start = ((f32[32,1,1152]{2,1,0:T(1,128)}), f32[32,1,1152]{2,1,0:T(1,128)S(1)}, u32[]{:S(2)}, u32[]{:S(2)}) async-start(f32[32,1,1152]{2,1,0:T(1,128)} %first_owner.1), calls=%async_computation | async-start | bytes 294912 | tf_op jit(solution)/shard_map/all_to_all | solution.py:827
  26.5 0.7 copy-start

commit v2 on v1

--- a/solution.py
+++ b/solution.py
@@ -177,19 +177,23 @@
         index = idx_ref[pl.ds(base, 8), :]
         high = index >> 7
         low = index & 127
-        highs = [jnp.broadcast_to(high[k : k + 1], (8, LANES)) for k in range(8)]
-        lows = [jnp.broadcast_to(low[k : k + 1], (8, LANES)) for k in range(8)]
-        totals = [jnp.zeros((8, LANES), f32) for k in range(9)]
+        totals = []
+        for k in range(8):
+            row_high = jnp.broadcast_to(high[k : k + 1], (8, LANES))
+            row_low = jnp.broadcast_to(low[k : k + 1], (8, LANES))
+            total = jnp.zeros((8, LANES), f32)
+            for chunk in range(chunks):
+                found = jnp.take_along_axis(
+                    main_ref[chunk], row_low, axis=1, mode="promise_in_bounds"
+                )
+                total = jnp.where(row_high == chunk, found, total)
+            totals.append(total)
+        total = jnp.zeros((8, LANES), f32)
         for chunk in range(chunks):
-            source = main_ref[chunk]
-            for k in range(8):
-                found = jnp.take_along_axis(
-                    source, lows[k], axis=1, mode="promise_in_bounds"
-                )
-                totals[k] = jnp.where(highs[k] == chunk, found, totals[k])
             source = jnp.broadcast_to(last_ref[chunk : chunk + 1, :], (8, LANES))
             found = jnp.take_along_axis(source, low, axis=1, mode="promise_in_bounds")
-            totals[8] = jnp.where(high == chunk, found, totals[8])
+            total = jnp.where(high == chunk, found, total)
+        totals.append(total)
         write(group, totals[:8], totals[8])
         return unused
 
@@ -639,8 +643,8 @@
             pair = pair_ref[span, :]
             high, low = split_colours(splat_ref, tile)
             rendered = colour_sum(high, low, pair)
-            wanted = targets_ref[tile]
-            wanted = jnp.concatenate([wanted, jnp.zeros((5, TILE_PIXELS), f32)], axis=0)
+            wanted = [targets_ref[channel, pl.ds(tile, 1), :] for channel in range(3)]
+            wanted = jnp.concatenate(wanted + [jnp.zeros((5, TILE_PIXELS), f32)], axis=0)
             delta = rendered - wanted
             delta_high = delta.astype(bf16).astype(f32)
             delta_low = delta - delta_high
@@ -793,7 +797,9 @@
             tile = first + k
             high, low = split_colours(splat_ref, tile)
             pair = pair_ref[k * TILE_PIXELS : (k + 1) * TILE_PIXELS, :]
-            out_ref[tile] = colour_sum(high, low, pair)[0:3]
+            rendered = colour_sum(high, low, pair)
+            for channel in range(3):
+                out_ref[channel, pl.ds(tile, 1), :] = rendered[channel : channel + 1]
         return unused
 
     lax.fori_loop(0, tile_count // batch, batch_step, 0)
@@ -805,7 +811,7 @@
     pixels = batch_tiles(tile_count) * TILE_PIXELS
     return pl.pallas_call(
         render_body,
-        out_shape=jax.ShapeDtypeStruct((tile_count, 3, TILE_PIXELS), f32),
+        out_shape=jax.ShapeDtypeStruct((3, tile_count, TILE_PIXELS), f32),
         in_specs=[SMEM, VMEM, VMEM],
         out_specs=VMEM,
         scratch_shapes=[
@@ -850,7 +856,7 @@
     half_height = 0.5 * (lists_first.shape[0] * devices // TILES_X * tile_edge)
     packed = first_owner(camera, gauss_params, send_first, half_width, half_height)
     packed = exchange(packed, devices)
-    packed = train(tiles_first, lists_first, targets, packed)
+    packed = train(tiles_first, lists_first, jnp.transpose(targets, (1, 0, 2)), packed)
     packed = exchange(packed, devices)
     new_params, new_first, new_second, packed = second_owner(
         camera,
@@ -865,7 +871,7 @@
     )
     packed = exchange(packed, devices)
     rendered = render(tiles_second, lists_second, packed)
-    return (new_params, new_first, new_second, rendered)
+    return (new_params, new_first, new_second, jnp.transpose(rendered, (1, 0, 2)))
 
 
 def solution(mesh):

time: 120 us -> 100 us (0.83)
  Pallas kernels: 77.5 us -> 60.1 us
  blocking collectives: 23.4 us -> 39.2 us
  waiting for transfers between devices: 7.68 us -> 0 us
  starting transfers between devices: 7.33 us -> 0 us
  local copies, waits for them, and re-layouts: 2.95 us -> 0 us
    all_to_all x2 -> x3, blocking collectives: 23.4 us -> 39.2 us  [exchange(): lax.all_to_all(packed, 'dev', split_axis=0, concat_axis=0, tiled=True)]
    pallas_call x1, Pallas kernels: 23.2 us -> 15.5 us  [second_owner(): pl.pallas_call(functools.partial(second_owner_body, half_width, half_heig...]
    all_to_all x1 -> x0, waiting for transfers between devices: 7.68 us -> none  [exchange(): lax.all_to_all(packed, 'dev', split_axis=0, concat_axis=0, tiled=True)]
    all_to_all x1 -> x0, starting transfers between devices: 7.33 us -> none  [exchange(): lax.all_to_all(packed, 'dev', split_axis=0, concat_axis=0, tiled=True)]
    pallas_call x1, Pallas kernels: 10.1 us -> 6.17 us  [first_owner(): pl.pallas_call(functools.partial(first_owner_body, half_width, half_heigh...]
    pallas_call x1, Pallas kernels: 29.6 us -> 25.8 us  [train(): pl.pallas_call(train_body, out_shape=jax.ShapeDtypeStruct(packed.shape, f...]
    unnamed x6 -> x0, local copies, waits for them, and re-layouts: 2.95 us -> none
    pallas_call x1, Pallas kernels: 14.5 us -> 12.6 us  [render(): pl.pallas_call(render_body, out_shape=jax.ShapeDtypeStruct((3, tile_count...]
  transfers between devices with their start and end apart: 1 -> 0, of which waited for: 1 -> 0; matrix products, arithmetic and copies ran while one was open for 1% -> 0% of each run, Pallas kernels for 0% -> 0%
where the time goes in v2:
time: 100 us
  Pallas kernels  60.1 us (60%)
  blocking collectives  39.2 us (39%)
    all_to_all x3, blocking collectives, exchange(): lax.all_to_all(packed, 'dev', split_axis=0, concat_axis=0, tiled=True)  39.2 us
    pallas_call x1, Pallas kernels, train(): pl.pallas_call(train_body, out_shape=jax.ShapeDtypeStruct(packed.shape, f...  25.8 us
    pallas_call x1, Pallas kernels, second_owner(): pl.pallas_call(functools.partial(second_owner_body, half_width, half_heig...  15.5 us
    pallas_call x1, Pallas kernels, render(): pl.pallas_call(render_body, out_shape=jax.ShapeDtypeStruct((3, tile_count...  12.6 us
    pallas_call x1, Pallas kernels, first_owner(): pl.pallas_call(functools.partial(first_owner_body, half_width, half_heigh...  6.17 us

profile of v2, /device:TPU:0, one launch (start us, length us, event | category | flops | bytes accessed | tf_op | source)
XLA Modules:
  0.0 100.0 jit_solution(17968418605241775096)
XLA Ops:
  0.6 6.2 %first_owner.1 = f32[32,1,1152]{2,1,0:T(1,128)} custom-call(f32[2,6]{1,0:T(2,128)} %camera_ref.3, f32[59,8192]{1,0:T(8,128)} %params_ref.3, s32[1,4096]{1,0:T(1,128)} %slots_ref.3), custom_call_target="tpu_custom_call" | custom-call | tf_op jit(solution)/shard_map/first_owner/pallas_call | solution.py:326
  6.8 15.8 %all_to_all.15.packed_ref = f32[32,1,1152]{2,1,0:T(1,128)} all-to-all(f32[32,1,1152]{2,1,0:T(1,128)} %first_owner.1), channel_id=1, replica_groups=mesh['dev'=32] {'dev'}, dimensions={0} | all-to-all | bytes 294912 | tf_op jit(solution)/shard_map/all_to_all | solution.py:833
  22.6 25.8 %train_tiles.1 = f32[32,1,1152]{2,1,0:T(1,128)} custom-call(s32[32]{0:T(128)} %numbers_ref.2, s32[32,128]{1,0:T(8,128)} %lists_ref.2, f32[3,32,256]{2,1,0:T(8,128)} %bitcast.2, f32[32,1,1152]{2,1,0:T(1,128)} %all_to_all.15.packed_ref), custom_call_target="tpu_custom_call" | custom-call | tf_op jit(solution)/shard_map/train_tiles/pallas_call | solution.py:736
  48.4 11.7 %all_to_all.16.packed_ref = f32[32,1,1152]{2,1,0:T(1,128)} all-to-all(f32[32,1,1152]{2,1,0:T(1,128)} %train_tiles.1), channel_id=1, replica_groups=mesh['dev'=32] {'dev'}, dimensions={0} | all-to-all | bytes 294912 | tf_op jit(solution)/shard_map/all_to_all | solution.py:833
  60.1 15.5 %second_owner.1 = (f32[59,8192]{1,0:T(8,128)}, f32[59,8192]{1,0:T(8,128)}, f32[59,8192]{1,0:T(8,128)}, f32[32,1,1152]{2,1,0:T(1,128)}) custom-call(f32[2,6]{1,0:T(2,128)} %camera_ref.3, f32[59,8192]{1,0:T(8,128)} %params_ref.3, f32[59,8192]{1,0:T(8,128)} %first_hbm.1, f32[59,8192]{1,0:T(8,128)} %second_hbm.1, s32[1,4096]{1,0:T(1,128)} %slots_ref.3, ...), custom_call_target="tpu_custom_call" | custom-call | tf_op jit(solution)/shard_map/second_owner/pallas_call | solution.py:467
  75.6 11.7 %all_to_all.17.packed_ref = f32[32,1,1152]{2,1,0:T(1,128)} all-to-all(f32[32,1,1152]{2,1,0:T(1,128)} %get-tuple-element.11), channel_id=1, replica_groups=mesh['dev'=32] {'dev'}, dimensions={0} | all-to-all | bytes 294912 | tf_op jit(solution)/shard_map/all_to_all | solution.py:833
  87.3 12.6 %render_tiles.1 = f32[3,32,256]{2,1,0:T(8,128)} custom-call(s32[32]{0:T(128)} %numbers_ref.3, s32[32,128]{1,0:T(8,128)} %lists_ref.3, f32[32,1,1152]{2,1,0:T(1,128)} %all_to_all.17.packed_ref), custom_call_target="tpu_custom_call" | custom-call | tf_op jit(solution)/shard_map/render_tiles/pallas_call | solution.py:812

commit v3 on v2

--- a/solution.py
+++ b/solution.py
@@ -15,6 +15,7 @@
 LANES = 128
 ROWS = 9
 STRIDE = 72
+PARTS = 4
 
 tile_edge = 16
 focal_length = 1000.0
@@ -325,7 +326,7 @@
     rows = slots.shape[1] // LANES
     return pl.pallas_call(
         functools.partial(first_owner_body, half_width, half_height),
-        out_shape=jax.ShapeDtypeStruct((rows, 1, ROWS * LANES), f32),
+        out_shape=pltpu.VMEM((rows, 1, ROWS * LANES), f32),
         in_specs=[SMEM, VMEM, VMEM],
         out_specs=VMEM,
         scratch_shapes=[
@@ -466,7 +467,7 @@
     shape = jax.ShapeDtypeStruct(params.shape, f32)
     return pl.pallas_call(
         functools.partial(second_owner_body, half_width, half_height),
-        out_shape=(shape, shape, shape, jax.ShapeDtypeStruct((rows, 1, ROWS * LANES), f32)),
+        out_shape=(shape, shape, shape, pltpu.VMEM((rows, 1, ROWS * LANES), f32)),
         in_specs=[SMEM, VMEM, ANY, ANY, VMEM, VMEM, VMEM],
         out_specs=(ANY, ANY, ANY, VMEM),
         scratch_shapes=[
@@ -504,6 +505,9 @@
     return 8 if tile_count % 8 == 0 else 1
 
 
+LOG2_E = 1.4426950408889634
+
+
 def tile_offsets(splat_ref, tile, number):
     left = (number % TILES_X) * tile_edge
     top = (number // TILES_X) * tile_edge
@@ -515,40 +519,44 @@
     return across, down
 
 
-def spread_row(ref, row):
-    return jnp.broadcast_to(ref[row : row + 1, :], (8, LANES))
-
-
-def alpha_phase(splat_ref, tile, number, base, row_ref, alpha_ref, odds_ref, pair_ref):
+def spread_row(ref, item, row):
+    return jnp.broadcast_to(ref[item, row : row + 1, :], (8, LANES))
+
+
+def alpha_phase(splat_ref, tile, number, item, row_ref, alpha_ref, odds_ref, pair_ref):
     a, b, c, o = [jnp.broadcast_to(splat_ref[tile, k : k + 1, :], (8, LANES)) for k in (2, 3, 4, 5)]
     across, down = tile_offsets(splat_ref, tile, number)
-    along = [(-0.5 * a) * x * x for x in across]
+    base = item * TILE_PIXELS
+    along = [((-0.5 * LOG2_E) * a) * x * x for x in across]
     for h in range(2):
-        row_ref[8 * h : 8 * h + 8, :] = (-0.5 * c) * down[h] * down[h]
-        row_ref[16 + 8 * h : 24 + 8 * h, :] = -(b * down[h])
+        row_ref[item, 8 * h : 8 * h + 8, :] = ((-0.5 * LOG2_E) * c) * down[h] * down[h]
+        row_ref[item, 16 + 8 * h : 24 + 8 * h, :] = ((-LOG2_E) * b) * down[h]
+        if odds_ref is not None:
+            row_ref[item, 32 + 8 * h : 40 + 8 * h, :] = down[h]
     for row in range(tile_edge):
-        fixed = spread_row(row_ref, row)
-        slope = spread_row(row_ref, 16 + row)
+        fixed = spread_row(row_ref, item, row)
+        slope = spread_row(row_ref, item, 16 + row)
         logs = []
         for h in range(2):
             exponent = along[h] + (fixed + slope * across[h])
-            alpha = o * jnp.exp(exponent)
-            log_clear = jnp.log(1.0 - alpha)
-            where = pl.ds(base + row * tile_edge + 8 * h, 8)
+            alpha = o * jnp.exp2(exponent)
+            log_clear = jnp.log(1.0 - alpha) * LOG2_E
+            where = slice(base + row * tile_edge + 8 * h, base + row * tile_edge + 8 * h + 8)
             alpha_ref[where, :] = alpha
             if odds_ref is not None:
-                odds_ref[where, :] = alpha * jnp.exp(-log_clear)
+                odds_ref[where, :] = alpha * jnp.exp2(-log_clear)
             logs.append(log_clear)
         high, low = halves(jnp.concatenate(logs, axis=0))
-        where = pl.ds(base + row * tile_edge, tile_edge)
+        where = slice(base + row * tile_edge, base + (row + 1) * tile_edge)
         pair_ref[where, :LIST_LEN] = high
         pair_ref[where, LIST_LEN:] = low
 
 
-def weight_phase(base, before_ref, alpha_ref, weight_ref, pair_ref):
+def weight_phase(item, before_ref, alpha_ref, weight_ref, pair_ref):
     for row in range(tile_edge):
-        where = pl.ds(base + row * tile_edge, tile_edge)
-        weight = alpha_ref[where, :] * jnp.exp(before_ref[where, :])
+        start = item * TILE_PIXELS + row * tile_edge
+        where = slice(start, start + tile_edge)
+        weight = alpha_ref[where, :] * jnp.exp2(before_ref[where, :])
         if weight_ref is not None:
             weight_ref[where, :] = weight
         high, low = halves(weight)
@@ -574,11 +582,7 @@
     return result[0:8] + result[8:16]
 
 
-def gather_tiles(lists_ref, packed_ref, main_ref, last_ref, splat_ref):
-    chunks = packed_ref.shape[0]
-    tile_count = lists_ref.shape[0]
-    unpack(packed_ref, main_ref, last_ref, chunks)
-
+def write_tiles(splat_ref):
     def write(group, vectors, last):
         for k in range(8):
             tile = group * 8 + k
@@ -586,7 +590,14 @@
             splat_ref[tile, 8:9, :] = last[k : k + 1]
             splat_ref[tile, 9:16, :] = jnp.zeros((7, LANES), f32)
 
-    permute(lists_ref, main_ref, last_ref, chunks, tile_count, write)
+    return write
+
+
+def staggered(stages, parts):
+    for turn in range(len(stages) + parts - 1):
+        for part in range(parts):
+            if 0 <= turn - part < len(stages):
+                stages[turn - part](part)
 
 
 def train_body(
@@ -601,121 +612,130 @@
     row_ref,
     alpha_ref,
     odds_ref,
-    plain_ref,
+    before_ref,
     weight_ref,
+    log_pair_ref,
     pair_ref,
+    pull_ref,
     grad_pair_ref,
     grad_ref,
     grad_last_ref,
     inverse_ref,
 ):
     tile_count = lists_ref.shape[0]
+    chunks = packed_ref.shape[0]
     batch = batch_tiles(tile_count)
-    gather_tiles(lists_ref, packed_ref, main_ref, last_ref, splat_ref)
-    invert(lists_ref, tile_count, packed_ref.shape[0], inverse_ref)
+    parts = PARTS if batch % PARTS == 0 else 1
+    size = batch // parts
+    unpack(packed_ref, main_ref, last_ref, chunks)
+    permute(lists_ref, main_ref, last_ref, chunks, tile_count, write_tiles(splat_ref))
+    invert(lists_ref, tile_count, chunks, inverse_ref)
     forward = triangle_pair(True)
     backward = triangle_pair(False)
 
     def batch_step(step, unused):
         first = step * batch
 
-        def alphas(k, unused):
-            tile = first + k
-            base = pl.multiple_of(k * TILE_PIXELS, TILE_PIXELS)
-            alpha_phase(
-                splat_ref, tile, numbers_ref[tile], base, row_ref, alpha_ref, odds_ref, pair_ref
+        def items(part):
+            return range(part * size, (part + 1) * size)
+
+        def span(part):
+            return slice(part * size * TILE_PIXELS, (part + 1) * size * TILE_PIXELS)
+
+        def alphas(part):
+            for item in items(part):
+                tile = first + item
+                alpha_phase(
+                    splat_ref, tile, numbers_ref[tile], item, row_ref, alpha_ref, odds_ref, log_pair_ref
+                )
+
+        def befores(part):
+            before_ref[span(part), :] = jnp.dot(
+                log_pair_ref[span(part), :], forward, preferred_element_type=f32
             )
-            return unused
-
-        lax.fori_loop(0, batch, alphas, 0)
-        plain_ref[...] = jnp.dot(pair_ref[...], forward, preferred_element_type=f32)
-
-        def weights(k, unused):
-            base = pl.multiple_of(k * TILE_PIXELS, TILE_PIXELS)
-            weight_phase(base, plain_ref, alpha_ref, weight_ref, pair_ref)
-            return unused
-
-        lax.fori_loop(0, batch, weights, 0)
-
-        for k in range(batch):
-            tile = first + k
-            span = slice(k * TILE_PIXELS, (k + 1) * TILE_PIXELS)
-            pair = pair_ref[span, :]
-            high, low = split_colours(splat_ref, tile)
-            rendered = colour_sum(high, low, pair)
-            wanted = [targets_ref[channel, pl.ds(tile, 1), :] for channel in range(3)]
-            wanted = jnp.concatenate(wanted + [jnp.zeros((5, TILE_PIXELS), f32)], axis=0)
-            delta = rendered - wanted
-            delta_high = delta.astype(bf16).astype(f32)
-            delta_low = delta - delta_high
-            left = jnp.concatenate(
-                [delta_high, delta_high, delta_low, jnp.zeros_like(delta)], axis=0
-            ).astype(bf16)
-            right = jnp.concatenate([high, low, high, jnp.zeros_like(high)], axis=0).astype(bf16)
-            plain_ref[span, :] = lax.dot_general(
-                left, right, (((0,), (0,)), ((), ())), preferred_element_type=f32
+
+        def weights(part):
+            for item in items(part):
+                weight_phase(item, before_ref, alpha_ref, weight_ref, pair_ref)
+
+        def deltas(part):
+            for item in items(part):
+                tile = first + item
+                pixels = slice(item * TILE_PIXELS, (item + 1) * TILE_PIXELS)
+                pair = pair_ref[pixels, :]
+                high, low = split_colours(splat_ref, tile)
+                rendered = colour_sum(high, low, pair)
+                wanted = [targets_ref[channel, pl.ds(tile, 1), :] for channel in range(3)]
+                wanted = jnp.concatenate(wanted + [jnp.zeros((5, TILE_PIXELS), f32)], axis=0)
+                delta = rendered - wanted
+                delta_high = delta.astype(bf16).astype(f32)
+                delta_low = delta - delta_high
+                left = jnp.concatenate(
+                    [delta_high, delta_high, delta_low, jnp.zeros_like(delta)], axis=0
+                ).astype(bf16)
+                right = jnp.concatenate([high, low, high, jnp.zeros_like(high)], axis=0).astype(bf16)
+                pulled = lax.dot_general(
+                    left, right, (((0,), (0,)), ((), ())), preferred_element_type=f32
+                )
+                for row in range(tile_edge):
+                    start = item * TILE_PIXELS + row * tile_edge
+                    where = slice(start, start + tile_edge)
+                    product = pulled[row * tile_edge : (row + 1) * tile_edge] * weight_ref[where, :]
+                    pull_ref[where, :] = product
+                    product_high, product_low = halves(product)
+                    grad_pair_ref[where, :LIST_LEN] = product_high
+                    grad_pair_ref[where, LIST_LEN:] = product_low
+                colour = jnp.dot(
+                    jnp.concatenate([delta_high, delta_low], axis=0).astype(bf16),
+                    pair,
+                    preferred_element_type=f32,
+                )
+                colour = colour[0:8, :LIST_LEN] + (colour[0:8, LIST_LEN:] + colour[8:16, :LIST_LEN])
+                grad_ref[tile, 6:8, :] = colour[0:2]
+                grad_last_ref[pl.ds(tile, 1), :] = colour[2:3]
+
+        def afters(part):
+            before_ref[span(part), :] = jnp.dot(
+                grad_pair_ref[span(part), :], backward, preferred_element_type=f32
             )
-            colour = jnp.dot(
-                jnp.concatenate([delta_high, delta_low], axis=0).astype(bf16),
-                pair,
-                preferred_element_type=f32,
-            )
-            colour = colour[0:8, :LIST_LEN] + (colour[0:8, LIST_LEN:] + colour[8:16, :LIST_LEN])
-            grad_ref[tile, 6:8, :] = colour[0:2]
-            grad_last_ref[pl.ds(tile, 1), :] = colour[2:3]
-
-        def pulls(k, unused):
-            for row in range(tile_edge):
-                where = pl.ds(pl.multiple_of(k * TILE_PIXELS, TILE_PIXELS) + row * tile_edge, tile_edge)
-                product = plain_ref[where, :] * weight_ref[where, :]
-                weight_ref[where, :] = product
-                high, low = halves(product)
-                grad_pair_ref[where, :LIST_LEN] = high
-                grad_pair_ref[where, LIST_LEN:] = low
-            return unused
-
-        lax.fori_loop(0, batch, pulls, 0)
-        plain_ref[...] = jnp.dot(grad_pair_ref[...], backward, preferred_element_type=f32)
-
-        def moments(k, unused):
-            tile = first + k
-            base = pl.multiple_of(k * TILE_PIXELS, TILE_PIXELS)
-            across, down = tile_offsets(splat_ref, tile, numbers_ref[tile])
-            for h in range(2):
-                row_ref[8 * h : 8 * h + 8, :] = down[h]
-            sums = [[jnp.zeros((8, LANES), f32) for j in range(3)] for h in range(2)]
-            for row in range(tile_edge):
-                offset = spread_row(row_ref, row)
-                for h in range(2):
-                    where = pl.ds(base + row * tile_edge + 8 * h, 8)
-                    slope = weight_ref[where, :] - plain_ref[where, :] * odds_ref[where, :]
-                    once = slope * offset
-                    sums[h][0] = sums[h][0] + slope
-                    sums[h][1] = sums[h][1] + once
-                    sums[h][2] = sums[h][2] + once * offset
-
-            def total(parts):
-                return jnp.sum(parts[0] + parts[1], axis=0, keepdims=True)
-
-            whole = total([sums[h][0] for h in range(2)])
-            along = [sums[h][0] * across[h] for h in range(2)]
-            moment_x = total(along)
-            moment_xx = total([along[h] * across[h] for h in range(2)])
-            moment_y = total([sums[h][1] for h in range(2)])
-            moment_xy = total([sums[h][1] * across[h] for h in range(2)])
-            moment_yy = total([sums[h][2] for h in range(2)])
-            a = splat_ref[tile, 2:3, :]
-            b = splat_ref[tile, 3:4, :]
-            c = splat_ref[tile, 4:5, :]
-            grad_ref[tile, 0:1, :] = -(a * moment_x + b * moment_y)
-            grad_ref[tile, 1:2, :] = -(c * moment_y + b * moment_x)
-            grad_ref[tile, 2:3, :] = -0.5 * moment_xx
-            grad_ref[tile, 3:4, :] = -moment_xy
-            grad_ref[tile, 4:5, :] = -0.5 * moment_yy
-            grad_ref[tile, 5:6, :] = whole
-            return unused
-
-        lax.fori_loop(0, batch, moments, 0)
+
+        def moments(part):
+            for item in items(part):
+                tile = first + item
+                across, down = tile_offsets(splat_ref, tile, numbers_ref[tile])
+                sums = [[jnp.zeros((8, LANES), f32) for j in range(3)] for h in range(2)]
+                for row in range(tile_edge):
+                    offset = spread_row(row_ref, item, 32 + row)
+                    for h in range(2):
+                        start = item * TILE_PIXELS + row * tile_edge + 8 * h
+                        where = slice(start, start + 8)
+                        slope = pull_ref[where, :] - before_ref[where, :] * odds_ref[where, :]
+                        once = slope * offset
+                        sums[h][0] = sums[h][0] + slope
+                        sums[h][1] = sums[h][1] + once
+                        sums[h][2] = sums[h][2] + once * offset
+
+                def total(pieces):
+                    return jnp.sum(pieces[0] + pieces[1], axis=0, keepdims=True)
+
+                whole = total([sums[h][0] for h in range(2)])
+                along = [sums[h][0] * across[h] for h in range(2)]
+                moment_x = total(along)
+                moment_xx = total([along[h] * across[h] for h in range(2)])
+                moment_y = total([sums[h][1] for h in range(2)])
+                moment_xy = total([sums[h][1] * across[h] for h in range(2)])
+                moment_yy = total([sums[h][2] for h in range(2)])
+                a = splat_ref[tile, 2:3, :]
+                b = splat_ref[tile, 3:4, :]
+                c = splat_ref[tile, 4:5, :]
+                grad_ref[tile, 0:1, :] = -(a * moment_x + b * moment_y)
+                grad_ref[tile, 1:2, :] = -(c * moment_y + b * moment_x)
+                grad_ref[tile, 2:3, :] = -0.5 * moment_xx
+                grad_ref[tile, 3:4, :] = -moment_xy
+                grad_ref[tile, 4:5, :] = -0.5 * moment_yy
+                grad_ref[tile, 5:6, :] = whole
+
+        staggered([alphas, befores, weights, deltas, afters, moments], parts)
         return unused
 
     lax.fori_loop(0, tile_count // batch, batch_step, 0)
@@ -732,23 +752,28 @@
 def train(numbers, lists, targets, packed):
     tile_count = lists.shape[0]
     chunks = packed.shape[0]
-    pixels = batch_tiles(tile_count) * TILE_PIXELS
+    batch = batch_tiles(tile_count)
+    pixels = batch * TILE_PIXELS
+    plain = pltpu.VMEM((pixels, LIST_LEN), f32)
+    pairs = pltpu.VMEM((pixels, 2 * LIST_LEN), bf16)
     return pl.pallas_call(
         train_body,
-        out_shape=jax.ShapeDtypeStruct(packed.shape, f32),
+        out_shape=pltpu.VMEM(packed.shape, f32),
         in_specs=[SMEM, VMEM, VMEM, VMEM],
         out_specs=VMEM,
         scratch_shapes=[
             pltpu.VMEM((chunks, 8, LANES), f32),
             pltpu.VMEM((chunks, LANES), f32),
             pltpu.VMEM((tile_count, 16, LANES), f32),
-            pltpu.VMEM((32, LANES), f32),
-            pltpu.VMEM((pixels, LIST_LEN), f32),
-            pltpu.VMEM((pixels, LIST_LEN), f32),
-            pltpu.VMEM((pixels, LIST_LEN), f32),
-            pltpu.VMEM((pixels, LIST_LEN), f32),
-            pltpu.VMEM((pixels, 2 * LIST_LEN), bf16),
-            pltpu.VMEM((pixels, 2 * LIST_LEN), bf16),
+            pltpu.VMEM((batch, 48, LANES), f32),
+            plain,
+            plain,
+            plain,
+            plain,
+            pairs,
+            pairs,
+            plain,
+            pairs,
             pltpu.VMEM((tile_count, 8, LANES), f32),
             pltpu.VMEM((tile_count, LANES), f32),
             pltpu.VMEM((chunks, LANES), jnp.int32),
@@ -767,39 +792,54 @@
     splat_ref,
     row_ref,
     alpha_ref,
-    plain_ref,
+    before_ref,
+    log_pair_ref,
     pair_ref,
 ):
     tile_count = lists_ref.shape[0]
+    chunks = packed_ref.shape[0]
     batch = batch_tiles(tile_count)
-    gather_tiles(lists_ref, packed_ref, main_ref, last_ref, splat_ref)
+    parts = PARTS if batch % PARTS == 0 else 1
+    size = batch // parts
+    unpack(packed_ref, main_ref, last_ref, chunks)
+    permute(lists_ref, main_ref, last_ref, chunks, tile_count, write_tiles(splat_ref))
     forward = triangle_pair(True)
 
     def batch_step(step, unused):
         first = step * batch
 
-        def alphas(k, unused):
-            tile = first + k
-            base = pl.multiple_of(k * TILE_PIXELS, TILE_PIXELS)
-            alpha_phase(splat_ref, tile, numbers_ref[tile], base, row_ref, alpha_ref, None, pair_ref)
-            return unused
-
-        lax.fori_loop(0, batch, alphas, 0)
-        plain_ref[...] = jnp.dot(pair_ref[...], forward, preferred_element_type=f32)
-
-        def weights(k, unused):
-            base = pl.multiple_of(k * TILE_PIXELS, TILE_PIXELS)
-            weight_phase(base, plain_ref, alpha_ref, None, pair_ref)
-            return unused
-
-        lax.fori_loop(0, batch, weights, 0)
-        for k in range(batch):
-            tile = first + k
-            high, low = split_colours(splat_ref, tile)
-            pair = pair_ref[k * TILE_PIXELS : (k + 1) * TILE_PIXELS, :]
-            rendered = colour_sum(high, low, pair)
-            for channel in range(3):
-                out_ref[channel, pl.ds(tile, 1), :] = rendered[channel : channel + 1]
+        def items(part):
+            return range(part * size, (part + 1) * size)
+
+        def span(part):
+            return slice(part * size * TILE_PIXELS, (part + 1) * size * TILE_PIXELS)
+
+        def alphas(part):
+            for item in items(part):
+                tile = first + item
+                alpha_phase(
+                    splat_ref, tile, numbers_ref[tile], item, row_ref, alpha_ref, None, log_pair_ref
+                )
+
+        def befores(part):
+            before_ref[span(part), :] = jnp.dot(
+                log_pair_ref[span(part), :], forward, preferred_element_type=f32
+            )
+
+        def weights(part):
+            for item in items(part):
+                weight_phase(item, before_ref, alpha_ref, None, pair_ref)
+
+        def colours(part):
+            for item in items(part):
+                tile = first + item
+                high, low = split_colours(splat_ref, tile)
+                pair = pair_ref[item * TILE_PIXELS : (item + 1) * TILE_PIXELS, :]
+                rendered = colour_sum(high, low, pair)
+                for channel in range(3):
+                    out_ref[channel, pl.ds(tile, 1), :] = rendered[channel : channel + 1]
+
+        staggered([alphas, befores, weights, colours], parts)
         return unused
 
     lax.fori_loop(0, tile_count // batch, batch_step, 0)
@@ -808,7 +848,10 @@
 def render(numbers, lists, packed):
     tile_count = lists.shape[0]
     chunks = packed.shape[0]
-    pixels = batch_tiles(tile_count) * TILE_PIXELS
+    batch = batch_tiles(tile_count)
+    pixels = batch * TILE_PIXELS
+    plain = pltpu.VMEM((pixels, LIST_LEN), f32)
+    pairs = pltpu.VMEM((pixels, 2 * LIST_LEN), bf16)
     return pl.pallas_call(
         render_body,
         out_shape=jax.ShapeDtypeStruct((3, tile_count, TILE_PIXELS), f32),
@@ -818,10 +861,11 @@
             pltpu.VMEM((chunks, 8, LANES), f32),
             pltpu.VMEM((chunks, LANES), f32),
             pltpu.VMEM((tile_count, 16, LANES), f32),
-            pltpu.VMEM((32, LANES), f32),
-            pltpu.VMEM((pixels, LIST_LEN), f32),
-            pltpu.VMEM((pixels, LIST_LEN), f32),
-            pltpu.VMEM((pixels, 2 * LIST_LEN), bf16),
+            pltpu.VMEM((batch, 48, LANES), f32),
+            plain,
+            plain,
+            pairs,
+            pairs,
         ],
         name="render_tiles",
     )(numbers, lists, packed)
@@ -830,7 +874,8 @@
 def exchange(packed, devices):
     rows = packed.shape[0]
     if rows == devices:
-        return lax.all_to_all(packed, "dev", split_axis=0, concat_axis=0, tiled=True)
+        packed = lax.all_to_all(packed, "dev", split_axis=0, concat_axis=0, tiled=True)
+        return pltpu.with_memory_space_constraint(packed, pltpu.VMEM)
     cap = rows * LANES // devices
     slots = packed.reshape(rows, ROWS, LANES).transpose(1, 0, 2).reshape(ROWS, devices, cap)
     slots = lax.all_to_all(slots, "dev", split_axis=1, concat_axis=1, tiled=True)

time: 100 us -> 78.6 us (0.79)
  Pallas kernels: 60.1 us -> 41.4 us
  blocking collectives: 39.2 us -> 36.2 us
    pallas_call x1, Pallas kernels: 25.8 us -> 14.5 us  [train(): pl.pallas_call(train_body, out_shape=pltpu.VMEM(packed.shape, f32), in_sp...]
    pallas_call x1, Pallas kernels: 12.6 us -> 6.57 us  [render(): pl.pallas_call(render_body, out_shape=jax.ShapeDtypeStruct((3, tile_count...]
    all_to_all x3, blocking collectives: 39.2 us -> 36.2 us  [exchange(): lax.all_to_all(packed, 'dev', split_axis=0, concat_axis=0, tiled=True)]
where the time goes in v3:
time: 78.6 us; the launch traced here: 78.3 us
  Pallas kernels  41.4 us (53%)
  blocking collectives  36.2 us (46%)
    all_to_all x3, blocking collectives, exchange(): lax.all_to_all(packed, 'dev', split_axis=0, concat_axis=0, tiled=True)  36.2 us
    pallas_call x1, Pallas kernels, second_owner(): pl.pallas_call(functools.partial(second_owner_body, half_width, half_heig...  14.9 us
    pallas_call x1, Pallas kernels, train(): pl.pallas_call(train_body, out_shape=pltpu.VMEM(packed.shape, f32), in_sp...  14.5 us
    pallas_call x1, Pallas kernels, render(): pl.pallas_call(render_body, out_shape=jax.ShapeDtypeStruct((3, tile_count...  6.57 us
    pallas_call x1, Pallas kernels, first_owner(): pl.pallas_call(functools.partial(first_owner_body, half_width, half_heigh...  5.5 us

profile of v3, /device:TPU:0, one launch (start us, length us, event | category | flops | bytes accessed | tf_op | source)
XLA Modules:
  0.0 78.3 jit_solution(18074324955775967157)
XLA Ops:
  0.6 5.5 %first_owner.1 = f32[32,1,1152]{2,1,0:T(1,128)S(1)} custom-call(f32[2,6]{1,0:T(2,128)} %camera_ref.3, f32[59,8192]{1,0:T(8,128)} %params_ref.3, s32[1,4096]{1,0:T(1,128)} %slots_ref.3), custom_call_target="tpu_custom_call" | custom-call | tf_op jit(solution)/shard_map/first_owner/pallas_call | solution.py:327
  6.1 15.5 %all_to_all.15.packed_ref = f32[32,1,1152]{2,1,0:T(1,128)S(1)} all-to-all(f32[32,1,1152]{2,1,0:T(1,128)S(1)} %first_owner.1), channel_id=1, replica_groups=mesh['dev'=32] {'dev'}, dimensions={0} | all-to-all | bytes 294912 | tf_op jit(solution)/shard_map/all_to_all | solution.py:877
  21.7 14.5 %train_tiles.1 = f32[32,1,1152]{2,1,0:T(1,128)S(1)} custom-call(s32[32]{0:T(128)} %numbers_ref.2, s32[32,128]{1,0:T(8,128)} %lists_ref.2, f32[3,32,256]{2,1,0:T(8,128)} %bitcast.2, f32[32,1,1152]{2,1,0:T(1,128)S(1)} %all_to_all.15.packed_ref), custom_call_target="tpu_custom_call" | custom-call | tf_op jit(solution)/shard_map/train_tiles/pallas_call | solution.py:759
  36.2 10.3 %all_to_all.16.packed_ref = f32[32,1,1152]{2,1,0:T(1,128)S(1)} all-to-all(f32[32,1,1152]{2,1,0:T(1,128)S(1)} %train_tiles.1), channel_id=1, replica_groups=mesh['dev'=32] {'dev'}, dimensions={0} | all-to-all | bytes 294912 | tf_op jit(solution)/shard_map/all_to_all | solution.py:877
  46.5 14.9 %second_owner.1 = (f32[59,8192]{1,0:T(8,128)}, f32[59,8192]{1,0:T(8,128)}, f32[59,8192]{1,0:T(8,128)}, f32[32,1,1152]{2,1,0:T(1,128)S(1)}) custom-call(f32[2,6]{1,0:T(2,128)} %camera_ref.3, f32[59,8192]{1,0:T(8,128)} %params_ref.3, f32[59,8192]{1,0:T(8,128)} %first_hbm.1, f32[59,8192]{1,0:T(8,128)} %second_hbm.1, s32[1,4096]{1,0:T(1,128)} %slots_ref.3, ...), custom_call_target="tpu_custom_call" | custom-call | tf_op jit(solution)/shard_map/second_owner/pallas_call | solution.py:468
  61.4 10.3 %all_to_all.17.packed_ref = f32[32,1,1152]{2,1,0:T(1,128)S(1)} all-to-all(f32[32,1,1152]{2,1,0:T(1,128)S(1)} %get-tuple-element.11), channel_id=1, replica_groups=mesh['dev'=32] {'dev'}, dimensions={0} | all-to-all | bytes 294912 | tf_op jit(solution)/shard_map/all_to_all | solution.py:877
  71.7 6.6 %render_tiles.1 = f32[3,32,256]{2,1,0:T(8,128)} custom-call(s32[32]{0:T(128)} %numbers_ref.3, s32[32,128]{1,0:T(8,128)} %lists_ref.3, f32[32,1,1152]{2,1,0:T(1,128)S(1)} %all_to_all.17.packed_ref), custom_call_target="tpu_custom_call" | custom-call | tf_op jit(solution)/shard_map/render_tiles/pallas_call | solution.py:855

commit v4 on v3

--- a/solution.py
+++ b/solution.py
@@ -16,6 +16,7 @@
 ROWS = 9
 STRIDE = 72
 PARTS = 4
+VMEM_LIMIT = 36 << 20
 
 tile_edge = 16
 focal_length = 1000.0
@@ -47,6 +48,7 @@
 VMEM = pl.BlockSpec(memory_space=pltpu.VMEM)
 SMEM = pl.BlockSpec(memory_space=pltpu.SMEM)
 ANY = pl.BlockSpec(memory_space=pl.ANY)
+HBM = pl.BlockSpec(memory_space=pltpu.HBM)
 
 
 def rate_values():
@@ -172,30 +174,33 @@
     ] + colours
 
 
+def permute_group(idx_ref, main_ref, last_ref, chunks, group, write):
+    base = pl.multiple_of(group * 8, 8)
+    index = idx_ref[pl.ds(base, 8), :]
+    high = index >> 7
+    low = index & 127
+    totals = []
+    for k in range(8):
+        row_high = jnp.broadcast_to(high[k : k + 1], (8, LANES))
+        row_low = jnp.broadcast_to(low[k : k + 1], (8, LANES))
+        total = jnp.zeros((8, LANES), f32)
+        for chunk in range(chunks):
+            found = jnp.take_along_axis(
+                main_ref[chunk], row_low, axis=1, mode="promise_in_bounds"
+            )
+            total = jnp.where(row_high == chunk, found, total)
+        totals.append(total)
+    total = jnp.zeros((8, LANES), f32)
+    for chunk in range(chunks):
+        source = jnp.broadcast_to(last_ref[chunk : chunk + 1, :], (8, LANES))
+        found = jnp.take_along_axis(source, low, axis=1, mode="promise_in_bounds")
+        total = jnp.where(high == chunk, found, total)
+    write(group, totals, total)
+
+
 def permute(idx_ref, main_ref, last_ref, chunks, rows, write):
     def group_step(group, unused):
-        base = pl.multiple_of(group * 8, 8)
-        index = idx_ref[pl.ds(base, 8), :]
-        high = index >> 7
-        low = index & 127
-        totals = []
-        for k in range(8):
-            row_high = jnp.broadcast_to(high[k : k + 1], (8, LANES))
-            row_low = jnp.broadcast_to(low[k : k + 1], (8, LANES))
-            total = jnp.zeros((8, LANES), f32)
-            for chunk in range(chunks):
-                found = jnp.take_along_axis(
-                    main_ref[chunk], row_low, axis=1, mode="promise_in_bounds"
-                )
-                total = jnp.where(row_high == chunk, found, total)
-            totals.append(total)
-        total = jnp.zeros((8, LANES), f32)
-        for chunk in range(chunks):
-            source = jnp.broadcast_to(last_ref[chunk : chunk + 1, :], (8, LANES))
-            found = jnp.take_along_axis(source, low, axis=1, mode="promise_in_bounds")
-            total = jnp.where(high == chunk, found, total)
-        totals.append(total)
-        write(group, totals[:8], totals[8])
+        permute_group(idx_ref, main_ref, last_ref, chunks, group, write)
         return unused
 
     lax.fori_loop(0, rows // 8, group_step, 0)
@@ -256,12 +261,13 @@
         idx_ref[row : row + 1, :] = slots_ref[:, row * LANES : (row + 1) * LANES]
 
 
-def to_dense(native, dense_ref, row_block, chunk):
+def native_to_group(native, ref, block, k):
     if native.shape[0] == 8:
-        dense_ref[pl.ds(8 * row_block * STRIDE + chunk, 8, stride=STRIDE), :] = native
+        ref[pl.ds(64 * block + k, 8, stride=8), :] = native
     else:
-        for k in range(native.shape[0]):
-            dense_ref[pl.ds((8 * row_block + k) * STRIDE + chunk, 1), :] = native[k : k + 1]
+        for row in range(native.shape[0]):
+            target = 64 * block + 8 * row + k
+            ref[target : target + 1, :] = native[row : row + 1]
 
 
 def dense_load(dense_ref, row, group):
@@ -274,16 +280,6 @@
 
 def row_blocks():
     return [(block, min(8, PARAMS - 8 * block)) for block in range((PARAMS + 7) // 8)]
-
-
-def project_groups(dense_ref, splat_ref, frame, half_width, half_height, chunks):
-    def step(group, unused):
-        params = [dense_load(dense_ref, row, group) for row in range(PARAMS)]
-        for row, value in enumerate(project(params, frame, half_width, half_height)):
-            dense_store(splat_ref, row, group, value)
-        return unused
-
-    lax.fori_loop(0, chunks // 8, step, 0)
 
 
 def send_splats(splat_ref, main_ref, idx_ref, packed_ref, chunks, rows):
@@ -296,28 +292,57 @@
 def first_owner_body(
     half_width,
     half_height,
-    camera_ref,
+    camera_hbm,
+    params_hbm,
+    slots_hbm,
+    packed_ref,
     params_ref,
     slots_ref,
-    packed_ref,
+    camera_ref,
     dense_ref,
     splat_ref,
     main_ref,
     idx_ref,
+    sems,
 ):
-    chunks = params_ref.shape[1] // LANES
-    rows = slots_ref.shape[1] // LANES
+    chunks = params_hbm.shape[1] // LANES
+    rows = slots_hbm.shape[1] // LANES
+    groups = chunks // 8
+    small = [
+        pltpu.make_async_copy(camera_hbm, camera_ref, sems.at[groups]),
+        pltpu.make_async_copy(slots_hbm, slots_ref, sems.at[groups + 1]),
+    ]
+
+    def load(group):
+        columns = pl.ds(pl.multiple_of(group * (8 * LANES), 8 * LANES), 8 * LANES)
+        return pltpu.make_async_copy(
+            params_hbm.at[:, columns], params_ref.at[:, columns], sems.at[group]
+        )
+
+    for copy in small:
+        copy.start()
+    for group in range(groups):
+        load(group).start()
+    for copy in small:
+        copy.wait()
+    frame = camera_frame(camera_ref, 0)
+
+    def step(group, unused):
+        load(group).wait()
+        for k in range(8):
+            chunk = group * 8 + k
+            lanes = pl.ds(pl.multiple_of(chunk * LANES, LANES), LANES)
+            for block, size in row_blocks():
+                native_to_group(
+                    params_ref[8 * block : 8 * block + size, lanes], dense_ref, block, k
+                )
+        params = [dense_ref[8 * row : 8 * row + 8, :] for row in range(PARAMS)]
+        for row, value in enumerate(project(params, frame, half_width, half_height)):
+            dense_store(splat_ref, row, group, value)
+        return unused
+
+    lax.fori_loop(0, groups, step, 0)
     slots_as_rows(slots_ref, idx_ref, rows)
-
-    def relayout(chunk, unused):
-        lanes = pl.ds(pl.multiple_of(chunk * LANES, LANES), LANES)
-        for block, size in row_blocks():
-            to_dense(params_ref[8 * block : 8 * block + size, lanes], dense_ref, block, chunk)
-        return unused
-
-    lax.fori_loop(0, chunks, relayout, 0, unroll=4)
-    frame = camera_frame(camera_ref, 0)
-    project_groups(dense_ref, splat_ref, frame, half_width, half_height, chunks)
     send_splats(splat_ref, main_ref, idx_ref, packed_ref, chunks, rows)
 
 
@@ -327,14 +352,19 @@
     return pl.pallas_call(
         functools.partial(first_owner_body, half_width, half_height),
         out_shape=pltpu.VMEM((rows, 1, ROWS * LANES), f32),
-        in_specs=[SMEM, VMEM, VMEM],
+        in_specs=[HBM, HBM, HBM],
         out_specs=VMEM,
         scratch_shapes=[
-            pltpu.VMEM((64 * STRIDE, LANES), f32),
+            pltpu.VMEM(params.shape, f32),
+            pltpu.VMEM(slots.shape, jnp.int32),
+            pltpu.SMEM(camera.shape, f32),
+            pltpu.VMEM((64 * 8, LANES), f32),
             pltpu.VMEM((ROWS * STRIDE, LANES), f32),
             pltpu.VMEM((chunks, 8, LANES), f32),
             pltpu.VMEM((rows, LANES), jnp.int32),
+            pltpu.SemaphoreType.DMA((chunks // 8 + 2,)),
         ],
+        compiler_params=pltpu.CompilerParams(vmem_limit_bytes=VMEM_LIMIT),
         name="first_owner",
     )(camera, params, slots)
 
@@ -355,48 +385,82 @@
     out_packed_ref,
     dense_ref,
     grad_ref,
+    fresh_ref,
     splat_ref,
+    next_splat_ref,
     main_ref,
     last_ref,
     idx_ref,
     inverse_ref,
-    params_out_ref,
     first_ref,
     second_ref,
+    params_out_ref,
+    first_out_ref,
+    second_out_ref,
     load_sems,
     store_sems,
 ):
     chunks = params_ref.shape[1] // LANES
     rows = slots_ref.shape[1] // LANES
-    loads = [
-        pltpu.make_async_copy(first_hbm, first_ref, load_sems.at[0]),
-        pltpu.make_async_copy(second_hbm, second_ref, load_sems.at[1]),
-    ]
-    for copy in loads:
-        copy.start()
+    groups = chunks // 8
+
+    def columns_of(group):
+        return pl.ds(pl.multiple_of(group * (8 * LANES), 8 * LANES), 8 * LANES)
+
+    def loads(group):
+        columns = columns_of(group)
+        return [
+            pltpu.make_async_copy(
+                source.at[:, columns], target.at[:, columns], load_sems.at[number, group]
+            )
+            for number, (source, target) in enumerate(
+                [(first_hbm, first_ref), (second_hbm, second_ref)]
+            )
+        ]
+
+    for group in range(groups):
+        for copy in loads(group):
+            copy.start()
     slots_as_rows(slots_ref, idx_ref, rows)
     invert(idx_ref, rows, chunks, inverse_ref)
     unpack(packed_ref, main_ref, last_ref, rows)
-
-    def relayout(chunk, unused):
-        lanes = pl.ds(pl.multiple_of(chunk * LANES, LANES), LANES)
-        for block, size in row_blocks():
-            to_dense(params_ref[8 * block : 8 * block + size, lanes], dense_ref, block, chunk)
-        return unused
-
-    lax.fori_loop(0, chunks, relayout, 0, unroll=4)
+    frame = camera_frame(camera_ref, 0)
+    next_frame = camera_frame(camera_ref, 1)
+    rates = rate_values() / bias_first
+    row_ids = lax.broadcasted_iota(jnp.int32, (8, LANES), 0)
 
     def write_columns(group, vectors, last):
         for k in range(8):
             splat_ref[pl.ds(group * 8 + k, 8, stride=STRIDE), :] = vectors[k]
         dense_store(splat_ref, 8, group, last)
 
-    permute(inverse_ref, main_ref, last_ref, rows, chunks, write_columns)
-
-    frame = camera_frame(camera_ref, 0)
-
-    def pull_step(group, unused):
-        params = [dense_load(dense_ref, row, group) for row in range(PARAMS)]
+    def lanes_of(group, k):
+        start = pl.multiple_of(group * (8 * LANES), 8 * LANES) + k * LANES
+        return pl.ds(pl.multiple_of(start, LANES), LANES)
+
+    def stores(group):
+        columns = columns_of(group)
+        return [
+            pltpu.make_async_copy(
+                source.at[:, columns], target.at[:, columns], store_sems.at[number, group]
+            )
+            for number, (source, target) in enumerate(
+                [
+                    (params_out_ref, out_params_hbm),
+                    (first_out_ref, out_first_hbm),
+                    (second_out_ref, out_second_hbm),
+                ]
+            )
+        ]
+
+    def work(group):
+        for copy in loads(group):
+            copy.wait()
+        for block, size in row_blocks():
+            for k in range(8):
+                native = params_ref[8 * block : 8 * block + size, lanes_of(group, k)]
+                native_to_group(native, dense_ref, block, k)
+        params = [dense_ref[8 * row : 8 * row + 8, :] for row in range(PARAMS)]
         splats, pullback = jax.vjp(
             lambda *p: project(list(p), frame, half_width, half_height), *params
         )
@@ -406,59 +470,47 @@
         grads = list(pullback(cotangents))
         grads[10] = through_opacity
         for row, value in enumerate(grads):
-            dense_store(grad_ref, row, group, value)
+            grad_ref[8 * row : 8 * row + 8, :] = value
+        for block, size in row_blocks():
+            span = slice(8 * block, 8 * block + size)
+            block_rates = rates[8 * block : 8 * block + 8]
+            step_size = jnp.full((8, LANES), block_rates[0], f32)
+            for k in range(1, 8):
+                if block_rates[k] != block_rates[0]:
+                    step_size = jnp.where(row_ids == k, f32(block_rates[k]), step_size)
+            step_size = step_size[:size]
+            for k in range(8):
+                lanes = lanes_of(group, k)
+                gradient = grad_ref[pl.ds(64 * block + k, 8, stride=8), :][:size]
+                moment = 0.9 * first_ref[span, lanes] + 0.1 * gradient
+                square = 0.999 * second_ref[span, lanes] + 0.001 * gradient * gradient
+                scaled = square * (1.0 / bias_second)
+                root = scaled * lax.rsqrt(scaled)
+                fresh = params_ref[span, lanes] - step_size * moment / (root + adam_epsilon)
+                first_out_ref[span, lanes] = moment
+                second_out_ref[span, lanes] = square
+                params_out_ref[span, lanes] = fresh
+                native_to_group(fresh, fresh_ref, block, k)
+        for copy in stores(group):
+            copy.start()
+        params = [fresh_ref[8 * row : 8 * row + 8, :] for row in range(PARAMS)]
+        for row, value in enumerate(project(params, next_frame, half_width, half_height)):
+            dense_store(next_splat_ref, row, group, value)
+
+    permute_group(inverse_ref, main_ref, last_ref, rows, 0, write_columns)
+
+    def step(group, unused):
+        work(group - 1)
+        permute_group(inverse_ref, main_ref, last_ref, rows, group, write_columns)
         return unused
 
-    lax.fori_loop(0, chunks // 8, pull_step, 0)
-
-    for copy in loads:
-        copy.wait()
-    rates = rate_values() / bias_first
-    stores = []
-    row_ids = lax.broadcasted_iota(jnp.int32, (8, LANES), 0)
-    for block, size in row_blocks():
-        span = slice(8 * block, 8 * block + size)
-        block_rates = rates[8 * block : 8 * block + 8]
-        step_size = jnp.full((8, LANES), block_rates[0], f32)
-        for k in range(1, 8):
-            if block_rates[k] != block_rates[0]:
-                step_size = jnp.where(row_ids == k, f32(block_rates[k]), step_size)
-        step_size = step_size[:size]
-
-        def adam_step(chunk, unused, block=block, size=size, span=span, step_size=step_size):
-            lanes = pl.ds(pl.multiple_of(chunk * LANES, LANES), LANES)
-            gradient = grad_ref[pl.ds(8 * block * STRIDE + chunk, 8, stride=STRIDE), :][:size]
-            moment = 0.9 * first_ref[span, lanes] + 0.1 * gradient
-            square = 0.999 * second_ref[span, lanes] + 0.001 * gradient * gradient
-            scaled = square * (1.0 / bias_second)
-            root = scaled * lax.rsqrt(scaled)
-            fresh = params_ref[span, lanes] - step_size * moment / (root + adam_epsilon)
-            first_ref[span, lanes] = moment
-            second_ref[span, lanes] = square
-            params_out_ref[span, lanes] = fresh
-            to_dense(fresh, dense_ref, block, chunk)
-            return unused
-
-        lax.fori_loop(0, chunks, adam_step, 0, unroll=8)
-        for number, (source, target) in enumerate(
-            [
-                (params_out_ref, out_params_hbm),
-                (first_ref, out_first_hbm),
-                (second_ref, out_second_hbm),
-            ]
-        ):
-            copy = pltpu.make_async_copy(
-                source.at[span, :], target.at[span, :], store_sems.at[number, block]
-            )
-            copy.start()
-            stores.append(copy)
-
+    lax.fori_loop(1, groups, step, 0)
+    work(groups - 1)
     slots_as_rows(next_slots_ref, idx_ref, rows)
-    frame = camera_frame(camera_ref, 1)
-    project_groups(dense_ref, splat_ref, frame, half_width, half_height, chunks)
-    send_splats(splat_ref, main_ref, idx_ref, out_packed_ref, chunks, rows)
-    for copy in stores:
-        copy.wait()
+    send_splats(next_splat_ref, main_ref, idx_ref, out_packed_ref, chunks, rows)
+    for group in range(groups):
+        for copy in stores(group):
+            copy.wait()
 
 
 def second_owner(camera, params, first, second, slots, next_slots, packed, half_width, half_height):
@@ -468,11 +520,13 @@
     return pl.pallas_call(
         functools.partial(second_owner_body, half_width, half_height),
         out_shape=(shape, shape, shape, pltpu.VMEM((rows, 1, ROWS * LANES), f32)),
-        in_specs=[SMEM, VMEM, ANY, ANY, VMEM, VMEM, VMEM],
+        in_specs=[SMEM, VMEM, HBM, HBM, VMEM, VMEM, VMEM],
         out_specs=(ANY, ANY, ANY, VMEM),
         scratch_shapes=[
-            pltpu.VMEM((64 * STRIDE, LANES), f32),
-            pltpu.VMEM((64 * STRIDE, LANES), f32),
+            pltpu.VMEM((64 * 8, LANES), f32),
+            pltpu.VMEM((64 * 8, LANES), f32),
+            pltpu.VMEM((64 * 8, LANES), f32),
+            pltpu.VMEM((ROWS * STRIDE, LANES), f32),
             pltpu.VMEM((ROWS * STRIDE, LANES), f32),
             pltpu.VMEM((max(chunks, rows), 8, LANES), f32),
             pltpu.VMEM((rows, LANES), f32),
@@ -481,9 +535,12 @@
             pltpu.VMEM(params.shape, f32),
             pltpu.VMEM(params.shape, f32),
             pltpu.VMEM(params.shape, f32),
-            pltpu.SemaphoreType.DMA((2,)),
-            pltpu.SemaphoreType.DMA((3, 8)),
+            pltpu.VMEM(params.shape, f32),
+            pltpu.VMEM(params.shape, f32),
+            pltpu.SemaphoreType.DMA((2, chunks // 8)),
+            pltpu.SemaphoreType.DMA((3, chunks // 8)),
         ],
+        compiler_params=pltpu.CompilerParams(vmem_limit_bytes=VMEM_LIMIT),
         name="second_owner",
     )(camera, params, first, second, slots, next_slots, packed)
 
@@ -502,7 +559,7 @@
 
 
 def batch_tiles(tile_count):
-    return 8 if tile_count % 8 == 0 else 1
+    return 8
 
 
 LOG2_E = 1.4426950408889634
@@ -628,12 +685,13 @@
     parts = PARTS if batch % PARTS == 0 else 1
     size = batch // parts
     unpack(packed_ref, main_ref, last_ref, chunks)
-    permute(lists_ref, main_ref, last_ref, chunks, tile_count, write_tiles(splat_ref))
+    write = write_tiles(splat_ref)
     invert(lists_ref, tile_count, chunks, inverse_ref)
+    permute_group(lists_ref, main_ref, last_ref, chunks, 0, write)
     forward = triangle_pair(True)
     backward = triangle_pair(False)
 
-    def batch_step(step, unused):
+    def work(step):
         first = step * batch
 
         def items(part):
@@ -736,9 +794,14 @@
                 grad_ref[tile, 5:6, :] = whole
 
         staggered([alphas, befores, weights, deltas, afters, moments], parts)
+
+    def batch_step(step, unused):
+        work(step - 1)
+        permute_group(lists_ref, main_ref, last_ref, chunks, step, write)
         return unused
 
-    lax.fori_loop(0, tile_count // batch, batch_step, 0)
+    lax.fori_loop(1, tile_count // batch, batch_step, 0)
+    work(tile_count // batch - 1)
     permute(
         inverse_ref,
         grad_ref,
@@ -778,6 +841,7 @@
             pltpu.VMEM((tile_count, LANES), f32),
             pltpu.VMEM((chunks, LANES), jnp.int32),
         ],
+        compiler_params=pltpu.CompilerParams(vmem_limit_bytes=VMEM_LIMIT),
         name="train_tiles",
     )(numbers, lists, targets, packed)
 
@@ -802,10 +866,11 @@
     parts = PARTS if batch % PARTS == 0 else 1
     size = batch // parts
     unpack(packed_ref, main_ref, last_ref, chunks)
-    permute(lists_ref, main_ref, last_ref, chunks, tile_count, write_tiles(splat_ref))
+    write = write_tiles(splat_ref)
+    permute_group(lists_ref, main_ref, last_ref, chunks, 0, write)
     forward = triangle_pair(True)
 
-    def batch_step(step, unused):
+    def work(step):
         first = step * batch
 
         def items(part):
@@ -840,9 +905,14 @@
                     out_ref[channel, pl.ds(tile, 1), :] = rendered[channel : channel + 1]
 
         staggered([alphas, befores, weights, colours], parts)
+
+    def batch_step(step, unused):
+        work(step - 1)
+        permute_group(lists_ref, main_ref, last_ref, chunks, step, write)
         return unused
 
-    lax.fori_loop(0, tile_count // batch, batch_step, 0)
+    lax.fori_loop(1, tile_count // batch, batch_step, 0)
+    work(tile_count // batch - 1)
 
 
 def render(numbers, lists, packed):
@@ -867,6 +937,7 @@
             pairs,
             pairs,
         ],
+        compiler_params=pltpu.CompilerParams(vmem_limit_bytes=VMEM_LIMIT),
         name="render_tiles",
     )(numbers, lists, packed)
 
@@ -899,23 +970,27 @@
     devices = lax.axis_size("dev")
     half_width = 0.5 * TILES_X * tile_edge
     half_height = 0.5 * (lists_first.shape[0] * devices // TILES_X * tile_edge)
-    packed = first_owner(camera, gauss_params, send_first, half_width, half_height)
+    keep = functools.partial(pltpu.with_memory_space_constraint, memory_space=pltpu.VMEM)
+    leave = functools.partial(pltpu.with_memory_space_constraint, memory_space=pltpu.HBM)
+    packed = first_owner(
+        leave(camera), leave(gauss_params), leave(send_first), half_width, half_height
+    )
     packed = exchange(packed, devices)
-    packed = train(tiles_first, lists_first, jnp.transpose(targets, (1, 0, 2)), packed)
+    packed = train(tiles_first, keep(lists_first), jnp.transpose(targets, (1, 0, 2)), packed)
     packed = exchange(packed, devices)
     new_params, new_first, new_second, packed = second_owner(
         camera,
-        gauss_params,
-        adam_first,
-        adam_second,
-        send_first,
-        send_second,
+        keep(gauss_params),
+        leave(adam_first),
+        leave(adam_second),
+        keep(send_first),
+        keep(send_second),
         packed,
         half_width,
         half_height,
     )
     packed = exchange(packed, devices)
-    rendered = render(tiles_second, lists_second, packed)
+    rendered = render(tiles_second, keep(lists_second), packed)
     return (new_params, new_first, new_second, jnp.transpose(rendered, (1, 0, 2)))
 
 

time: 78.6 us -> 70.8 us (0.901)
  Pallas kernels: 41.4 us -> 33.6 us
    pallas_call x1, Pallas kernels: 14.9 us -> 10.4 us  [second_owner(): pl.pallas_call(functools.partial(second_owner_body, half_width, half_heig...]
    pallas_call x1, Pallas kernels: 14.5 us -> 12.6 us  [train(): pl.pallas_call(train_body, out_shape=pltpu.VMEM(packed.shape, f32), in_sp...]
    pallas_call x1, Pallas kernels: 6.57 us -> 5.56 us  [render(): pl.pallas_call(render_body, out_shape=jax.ShapeDtypeStruct((3, tile_count...]
where the time goes in v4:
time: 70.8 us; the launch traced here: 70.6 us
  blocking collectives  36.2 us (51%)
  Pallas kernels  33.6 us (47%)
  between operations  0.74 us (1%)
    all_to_all x3, blocking collectives, exchange(): lax.all_to_all(packed, 'dev', split_axis=0, concat_axis=0, tiled=True)  36.2 us
    pallas_call x1, Pallas kernels, train(): pl.pallas_call(train_body, out_shape=pltpu.VMEM(packed.shape, f32), in_sp...  12.6 us
    pallas_call x1, Pallas kernels, second_owner(): pl.pallas_call(functools.partial(second_owner_body, half_width, half_heig...  10.4 us
    pallas_call x1, Pallas kernels, render(): pl.pallas_call(render_body, out_shape=jax.ShapeDtypeStruct((3, tile_count...  5.56 us
    pallas_call x1, Pallas kernels, first_owner(): pl.pallas_call(functools.partial(first_owner_body, half_width, half_heigh...  5.07 us

profile of v4, /device:TPU:0, one launch (start us, length us, event | category | flops | bytes accessed | tf_op | source)
XLA Modules:
  0.0 70.6 jit_solution(3034407047269896048)
XLA Ops:
  0.6 0.0 copy-start.2
  0.6 0.0 copy-start.6
  0.7 0.0 copy-start
  0.7 0.0 copy-start.1
  0.7 0.0 copy-start.7
  0.7 0.0 copy-start.4
  0.7 0.0 copy-start.3
  0.7 5.1 %first_owner.1 = f32[32,1,1152]{2,1,0:T(1,128)S(1)} custom-call(f32[2,6]{1,0:T(2,128)} %camera_ref.1, f32[59,8192]{1,0:T(8,128)} %params_ref.1, s32[1,4096]{1,0:T(1,128)} %slots_ref.1), custom_call_target="tpu_custom_call" | custom-call | tf_op jit(solution)/shard_map/first_owner/pallas_call | solution.py:352
  5.8 15.5 %all_to_all.15.packed_ref = f32[32,1,1152]{2,1,0:T(1,128)S(1)} all-to-all(f32[32,1,1152]{2,1,0:T(1,128)S(1)} %first_owner.1), channel_id=1, replica_groups=mesh['dev'=32] {'dev'}, dimensions={0} | all-to-all | bytes 294912 | tf_op jit(solution)/shard_map/all_to_all | solution.py:948
  21.3 0.0 copy-done.1
  21.3 0.0 copy-done.7
  21.3 0.0 copy-done.4
  21.3 12.6 %train_tiles.1 = f32[32,1,1152]{2,1,0:T(1,128)S(1)} custom-call(s32[32]{0:T(128)S(1)} %copy-done.7, s32[32,128]{1,0:T(8,128)S(1)} %copy-done.4, f32[3,32,256]{2,1,0:T(8,128)S(1)} %bitcast.2, f32[32,1,1152]{2,1,0:T(1,128)S(1)} %all_to_all.15.packed_ref), custom_call_target="tpu_custom_call" | custom-call | tf_op jit(solution)/shard_map/train_tiles/pallas_call | solution.py:822
  33.9 10.3 %all_to_all.16.packed_ref = f32[32,1,1152]{2,1,0:T(1,128)S(1)} all-to-all(f32[32,1,1152]{2,1,0:T(1,128)S(1)} %train_tiles.1), channel_id=1, replica_groups=mesh['dev'=32] {'dev'}, dimensions={0} | all-to-all | bytes 294912 | tf_op jit(solution)/shard_map/all_to_all | solution.py:948
  44.3 0.0 copy-done.2
  44.3 0.0 copy-done.6
  44.3 0.0 copy-done
  44.3 0.0 copy-done.3
  44.3 0.0 copy-start.5
  44.3 0.0 copy-start.8
  44.3 10.4 %second_owner.1 = (f32[59,8192]{1,0:T(8,128)}, f32[59,8192]{1,0:T(8,128)}, f32[59,8192]{1,0:T(8,128)}, f32[32,1,1152]{2,1,0:T(1,128)S(1)}) custom-call(f32[2,6]{1,0:T(2,128)S(1)} %copy-done.6, f32[59,8192]{1,0:T(8,128)S(1)} %copy-done, f32[59,8192]{1,0:T(8,128)} %first_hbm.1, f32[59,8192]{1,0:T(8,128)} %second_hbm.1, s32[1,4096]{1,0:T(1,128)S(1)} %copy-done.2, ...), custom_call_target="tpu_custom_call" | custom-call | tf_op jit(solution)/shard_map/second_owner/pallas_call | solution.py:520
  54.7 10.3 %all_to_all.17.packed_ref = f32[32,1,1152]{2,1,0:T(1,128)S(1)} all-to-all(f32[32,1,1152]{2,1,0:T(1,128)S(1)} %get-tuple-element.11), channel_id=1, replica_groups=mesh['dev'=32] {'dev'}, dimensions={0} | all-to-all | bytes 294912 | tf_op jit(solution)/shard_map/all_to_all | solution.py:948
  65.0 0.0 copy-done.5
  65.0 5.6 %render_tiles.1 = f32[3,32,256]{2,1,0:T(8,128)} custom-call(s32[32]{0:T(128)S(1)} %copy-done.8, s32[32,128]{1,0:T(8,128)S(1)} %copy-done.5, f32[32,1,1152]{2,1,0:T(1,128)S(1)} %all_to_all.17.packed_ref), custom_call_target="tpu_custom_call" | custom-call | tf_op jit(solution)/shard_map/render_tiles/pallas_call | solution.py:925
  (1 shorter events, 0.0 us)
Async XLA Ops:
  0.6 43.6 %copy-start.2 = (s32[1,4096]{1,0:T(1,128)S(1)}, s32[1,4096]{1,0:T(1,128)}, u32[]{:S(2)}) copy-start(s32[1,4096]{1,0:T(1,128)} %slots_ref.1) | copy-start | bytes 49156
  0.6 43.6 %copy-start.6 = (f32[2,6]{1,0:T(2,128)S(1)}, f32[2,6]{1,0:T(2,128)}, u32[]{:S(2)}) copy-start(f32[2,6]{1,0:T(2,128)} %camera_ref.1) | copy-start | bytes 148
  0.7 43.6 %copy-start = (f32[59,8192]{1,0:T(8,128)S(1)}, f32[59,8192]{1,0:T(8,128)}, u32[]{:S(2)}) copy-start(f32[59,8192]{1,0:T(8,128)} %params_ref.1) | copy-start | bytes 5799940
  0.7 20.7 %copy-start.1 = (f32[32,3,256]{2,0,1:T(8,128)S(1)}, f32[32,3,256]{2,0,1:T(8,128)}, u32[]{:S(2)}) copy-start(f32[32,3,256]{2,0,1:T(8,128)} %param.21) | copy-start | bytes 294916
  0.7 20.7 %copy-start.7 = (s32[32]{0:T(128)S(1)}, s32[32]{0:T(128)}, u32[]{:S(2)}) copy-start(s32[32]{0:T(128)} %numbers_ref.2) | copy-start | bytes 388
  0.7 20.6 %copy-start.4 = (s32[32,128]{1,0:T(8,128)S(1)}, s32[32,128]{1,0:T(8,128)}, u32[]{:S(2)}) copy-start(s32[32,128]{1,0:T(8,128)} %lists_ref.2) | copy-start | bytes 49156
  0.7 43.6 %copy-start.3 = (s32[1,4096]{1,0:T(1,128)S(1)}, s32[1,4096]{1,0:T(1,128)}, u32[]{:S(2)}) copy-start(s32[1,4096]{1,0:T(1,128)} %next_slots_ref.1) | copy-start | bytes 49156
  44.3 20.7 %copy-start.5 = (s32[32,128]{1,0:T(8,128)S(1)}, s32[32,128]{1,0:T(8,128)}, u32[]{:S(2)}) copy-start(s32[32,128]{1,0:T(8,128)} %lists_ref.3) | copy-start | bytes 49156
  44.3 20.7 %copy-start.8 = (s32[32]{0:T(128)S(1)}, s32[32]{0:T(128)}, u32[]{:S(2)}) copy-start(s32[32]{0:T(128)} %numbers_ref.3) | copy-start | bytes 388

commit v5 on v4

--- a/solution.py
+++ b/solution.py
@@ -16,6 +16,7 @@
 ROWS = 9
 STRIDE = 72
 PARTS = 4
+BUFFERS = 2
 VMEM_LIMIT = 36 << 20
 
 tile_edge = 16
@@ -175,7 +176,7 @@
 
 
 def permute_group(idx_ref, main_ref, last_ref, chunks, group, write):
-    base = pl.multiple_of(group * 8, 8)
+    base = group * 8 if isinstance(group, int) else pl.multiple_of(group * 8, 8)
     index = idx_ref[pl.ds(base, 8), :]
     high = index >> 7
     low = index & 127
@@ -282,11 +283,60 @@
     return [(block, min(8, PARAMS - 8 * block)) for block in range((PARAMS + 7) // 8)]
 
 
-def send_splats(splat_ref, main_ref, idx_ref, packed_ref, chunks, rows):
+def split_splats(splat_ref, parts_ref, chunks):
+    for row in range(ROWS):
+        for start in range(0, chunks, 16):
+            value = splat_ref[row * STRIDE + start : row * STRIDE + start + 16, :]
+            target = slice(row * chunks + start, row * chunks + start + 16)
+            for term in range(3):
+                rounded = value.astype(bf16)
+                parts_ref[target, term * LANES : (term + 1) * LANES] = rounded
+                value = value - rounded.astype(f32)
+
+
+def matrix_gather(parts_ref, idx_ref, base, chunks, packed_ref):
+    index = idx_ref[pl.ds(pl.multiple_of(base, 8), 8), :]
+    high = index >> 7
+    low = index & 127
+    low_ids = lax.broadcasted_iota(jnp.int32, (LANES, LANES), 0)
+    ids = lax.broadcasted_iota(jnp.int32, (8, LANES), 0)
+    for pair in range(4):
+        rows = (2 * pair, 2 * pair + 1)
+        chosen = jnp.concatenate(
+            [jnp.where(low[row : row + 1] == low_ids, 1.0, 0.0) for row in rows], axis=1
+        ).astype(bf16)
+        found = jnp.dot(
+            parts_ref[...],
+            jnp.concatenate([chosen, chosen, chosen], axis=0),
+            preferred_element_type=f32,
+        )
+        for half, row in enumerate(rows):
+            wanted = jnp.broadcast_to(high[row : row + 1], (8, LANES))
+            masks = [ids + 8 * block == wanted for block in range(chunks // 8)]
+            for item in range(ROWS):
+                total = jnp.zeros((8, LANES), f32)
+                for block in range(chunks // 8):
+                    start = item * chunks + 8 * block
+                    piece = found[start : start + 8, half * LANES : (half + 1) * LANES]
+                    total = jnp.where(masks[block], piece, total)
+                packed_ref[base + row, :, item * LANES : (item + 1) * LANES] = jnp.sum(
+                    total, axis=0, keepdims=True
+                )
+
+
+def send_splats(splat_ref, main_ref, parts_ref, idx_ref, packed_ref, chunks, rows):
     for chunk in range(chunks):
         main_ref[chunk] = splat_ref[pl.ds(chunk, 8, stride=STRIDE), :]
     last_ref = splat_ref.at[pl.ds(8 * STRIDE, chunks), :]
-    permute(idx_ref, main_ref, last_ref, chunks, rows, pack_group(packed_ref))
+    split_splats(splat_ref, parts_ref, chunks)
+    write = pack_group(packed_ref)
+
+    def step(group, unused):
+        matrix_gather(parts_ref, idx_ref, rows // 2 + 8 * group, chunks, packed_ref)
+        permute_group(idx_ref, main_ref, last_ref, chunks, group, write)
+        return unused
+
+    lax.fori_loop(0, rows // 16, step, 0)
 
 
 def first_owner_body(
@@ -299,9 +349,11 @@
     params_ref,
     slots_ref,
     camera_ref,
-    dense_ref,
+    even_ref,
+    odd_ref,
     splat_ref,
     main_ref,
+    parts_ref,
     idx_ref,
     sems,
 ):
@@ -327,8 +379,7 @@
         copy.wait()
     frame = camera_frame(camera_ref, 0)
 
-    def step(group, unused):
-        load(group).wait()
+    def prepare(group, dense_ref):
         for k in range(8):
             chunk = group * 8 + k
             lanes = pl.ds(pl.multiple_of(chunk * LANES, LANES), LANES)
@@ -339,11 +390,17 @@
         params = [dense_ref[8 * row : 8 * row + 8, :] for row in range(PARAMS)]
         for row, value in enumerate(project(params, frame, half_width, half_height)):
             dense_store(splat_ref, row, group, value)
+
+    def step(pair, unused):
+        load(2 * pair).wait()
+        load(2 * pair + 1).wait()
+        prepare(2 * pair, even_ref)
+        prepare(2 * pair + 1, odd_ref)
         return unused
 
-    lax.fori_loop(0, groups, step, 0)
+    lax.fori_loop(0, groups // 2, step, 0)
     slots_as_rows(slots_ref, idx_ref, rows)
-    send_splats(splat_ref, main_ref, idx_ref, packed_ref, chunks, rows)
+    send_splats(splat_ref, main_ref, parts_ref, idx_ref, packed_ref, chunks, rows)
 
 
 def first_owner(camera, params, slots, half_width, half_height):
@@ -351,16 +408,17 @@
     rows = slots.shape[1] // LANES
     return pl.pallas_call(
         functools.partial(first_owner_body, half_width, half_height),
-        out_shape=pltpu.VMEM((rows, 1, ROWS * LANES), f32),
+        out_shape=(pltpu.VMEM((rows, 1, ROWS * LANES), f32), pltpu.VMEM(params.shape, f32)),
         in_specs=[HBM, HBM, HBM],
-        out_specs=VMEM,
+        out_specs=(VMEM, VMEM),
         scratch_shapes=[
-            pltpu.VMEM(params.shape, f32),
             pltpu.VMEM(slots.shape, jnp.int32),
             pltpu.SMEM(camera.shape, f32),
             pltpu.VMEM((64 * 8, LANES), f32),
+            pltpu.VMEM((64 * 8, LANES), f32),
             pltpu.VMEM((ROWS * STRIDE, LANES), f32),
             pltpu.VMEM((chunks, 8, LANES), f32),
+            pltpu.VMEM((ROWS * chunks, 3 * LANES), bf16),
             pltpu.VMEM((rows, LANES), jnp.int32),
             pltpu.SemaphoreType.DMA((chunks // 8 + 2,)),
         ],
@@ -389,6 +447,7 @@
     splat_ref,
     next_splat_ref,
     main_ref,
+    parts_ref,
     last_ref,
     idx_ref,
     inverse_ref,
@@ -507,7 +566,7 @@
     lax.fori_loop(1, groups, step, 0)
     work(groups - 1)
     slots_as_rows(next_slots_ref, idx_ref, rows)
-    send_splats(next_splat_ref, main_ref, idx_ref, out_packed_ref, chunks, rows)
+    send_splats(next_splat_ref, main_ref, parts_ref, idx_ref, out_packed_ref, chunks, rows)
     for group in range(groups):
         for copy in stores(group):
             copy.wait()
@@ -529,6 +588,7 @@
             pltpu.VMEM((ROWS * STRIDE, LANES), f32),
             pltpu.VMEM((ROWS * STRIDE, LANES), f32),
             pltpu.VMEM((max(chunks, rows), 8, LANES), f32),
+            pltpu.VMEM((ROWS * chunks, 3 * LANES), bf16),
             pltpu.VMEM((rows, LANES), f32),
             pltpu.VMEM((rows, LANES), jnp.int32),
             pltpu.VMEM((chunks, LANES), jnp.int32),
@@ -676,7 +736,7 @@
     pull_ref,
     grad_pair_ref,
     grad_ref,
-    grad_last_ref,
+    parts_ref,
     inverse_ref,
 ):
     tile_count = lists_ref.shape[0]
@@ -691,14 +751,19 @@
     forward = triangle_pair(True)
     backward = triangle_pair(False)
 
+    def put(item, tile, value):
+        grad_ref[pl.ds(item * STRIDE + tile, 1), :] = value
+
     def work(step):
-        first = step * batch
+        slot = (step % BUFFERS) * batch if isinstance(step, int) else 0
+        first = step * batch - slot
 
         def items(part):
-            return range(part * size, (part + 1) * size)
+            return range(slot + part * size, slot + (part + 1) * size)
 
         def span(part):
-            return slice(part * size * TILE_PIXELS, (part + 1) * size * TILE_PIXELS)
+            start = (slot + part * size) * TILE_PIXELS
+            return slice(start, start + size * TILE_PIXELS)
 
         def alphas(part):
             for item in items(part):
@@ -717,40 +782,54 @@
                 weight_phase(item, before_ref, alpha_ref, weight_ref, pair_ref)
 
         def deltas(part):
-            for item in items(part):
-                tile = first + item
-                pixels = slice(item * TILE_PIXELS, (item + 1) * TILE_PIXELS)
-                pair = pair_ref[pixels, :]
-                high, low = split_colours(splat_ref, tile)
-                rendered = colour_sum(high, low, pair)
-                wanted = [targets_ref[channel, pl.ds(tile, 1), :] for channel in range(3)]
-                wanted = jnp.concatenate(wanted + [jnp.zeros((5, TILE_PIXELS), f32)], axis=0)
-                delta = rendered - wanted
-                delta_high = delta.astype(bf16).astype(f32)
-                delta_low = delta - delta_high
-                left = jnp.concatenate(
-                    [delta_high, delta_high, delta_low, jnp.zeros_like(delta)], axis=0
-                ).astype(bf16)
-                right = jnp.concatenate([high, low, high, jnp.zeros_like(high)], axis=0).astype(bf16)
+            members = items(part)
+            for start in range(0, len(members), 2):
+                pair_items = members[start : start + 2]
+                lefts = []
+                rights = []
+                for place, item in enumerate(pair_items):
+                    tile = first + item
+                    pixels = slice(item * TILE_PIXELS, (item + 1) * TILE_PIXELS)
+                    pair = pair_ref[pixels, :]
+                    high, low = split_colours(splat_ref, tile)
+                    rendered = colour_sum(high, low, pair)
+                    wanted = [targets_ref[channel, pl.ds(tile, 1), :] for channel in range(3)]
+                    wanted = jnp.concatenate(wanted + [jnp.zeros((5, TILE_PIXELS), f32)], axis=0)
+                    delta = rendered - wanted
+                    delta_high = delta.astype(bf16).astype(f32)
+                    delta_low = delta - delta_high
+                    lefts += [delta_high, delta_high, delta_low, jnp.zeros_like(delta)]
+                    right = jnp.concatenate([high, low, high, jnp.zeros_like(high)], axis=0)
+                    blank = [jnp.zeros_like(right)] * len(pair_items)
+                    blank[place] = right
+                    rights.append(jnp.concatenate(blank, axis=1))
+                    colour = jnp.dot(
+                        jnp.concatenate([delta_high, delta_low], axis=0).astype(bf16),
+                        pair,
+                        preferred_element_type=f32,
+                    )
+                    colour = colour[0:8, :LIST_LEN] + (
+                        colour[0:8, LIST_LEN:] + colour[8:16, :LIST_LEN]
+                    )
+                    for channel in range(3):
+                        put(6 + channel, tile, colour[channel : channel + 1])
                 pulled = lax.dot_general(
-                    left, right, (((0,), (0,)), ((), ())), preferred_element_type=f32
-                )
-                for row in range(tile_edge):
-                    start = item * TILE_PIXELS + row * tile_edge
-                    where = slice(start, start + tile_edge)
-                    product = pulled[row * tile_edge : (row + 1) * tile_edge] * weight_ref[where, :]
-                    pull_ref[where, :] = product
-                    product_high, product_low = halves(product)
-                    grad_pair_ref[where, :LIST_LEN] = product_high
-                    grad_pair_ref[where, LIST_LEN:] = product_low
-                colour = jnp.dot(
-                    jnp.concatenate([delta_high, delta_low], axis=0).astype(bf16),
-                    pair,
+                    jnp.concatenate(lefts, axis=0).astype(bf16),
+                    jnp.concatenate(rights, axis=0).astype(bf16),
+                    (((0,), (0,)), ((), ())),
                     preferred_element_type=f32,
                 )
-                colour = colour[0:8, :LIST_LEN] + (colour[0:8, LIST_LEN:] + colour[8:16, :LIST_LEN])
-                grad_ref[tile, 6:8, :] = colour[0:2]
-                grad_last_ref[pl.ds(tile, 1), :] = colour[2:3]
+                for place, item in enumerate(pair_items):
+                    lanes = slice(place * LIST_LEN, (place + 1) * LIST_LEN)
+                    for row in range(tile_edge):
+                        begin = item * TILE_PIXELS + row * tile_edge
+                        where = slice(begin, begin + tile_edge)
+                        factor = pulled[row * tile_edge : (row + 1) * tile_edge, lanes]
+                        product = factor * weight_ref[where, :]
+                        pull_ref[where, :] = product
+                        product_high, product_low = halves(product)
+                        grad_pair_ref[where, :LIST_LEN] = product_high
+                        grad_pair_ref[where, LIST_LEN:] = product_low
 
         def afters(part):
             before_ref[span(part), :] = jnp.dot(
@@ -786,12 +865,12 @@
                 a = splat_ref[tile, 2:3, :]
                 b = splat_ref[tile, 3:4, :]
                 c = splat_ref[tile, 4:5, :]
-                grad_ref[tile, 0:1, :] = -(a * moment_x + b * moment_y)
-                grad_ref[tile, 1:2, :] = -(c * moment_y + b * moment_x)
-                grad_ref[tile, 2:3, :] = -0.5 * moment_xx
-                grad_ref[tile, 3:4, :] = -moment_xy
-                grad_ref[tile, 4:5, :] = -0.5 * moment_yy
-                grad_ref[tile, 5:6, :] = whole
+                put(0, tile, -(a * moment_x + b * moment_y))
+                put(1, tile, -(c * moment_y + b * moment_x))
+                put(2, tile, -0.5 * moment_xx)
+                put(3, tile, -moment_xy)
+                put(4, tile, -0.5 * moment_yy)
+                put(5, tile, whole)
 
         staggered([alphas, befores, weights, deltas, afters, moments], parts)
 
@@ -802,13 +881,8 @@
 
     lax.fori_loop(1, tile_count // batch, batch_step, 0)
     work(tile_count // batch - 1)
-    permute(
-        inverse_ref,
-        grad_ref,
-        grad_last_ref,
-        tile_count,
-        out_packed_ref.shape[0],
-        pack_group(out_packed_ref),
+    send_splats(
+        grad_ref, main_ref, parts_ref, inverse_ref, out_packed_ref, tile_count, chunks
     )
 
 
@@ -816,7 +890,7 @@
     tile_count = lists.shape[0]
     chunks = packed.shape[0]
     batch = batch_tiles(tile_count)
-    pixels = batch * TILE_PIXELS
+    pixels = BUFFERS * batch * TILE_PIXELS
     plain = pltpu.VMEM((pixels, LIST_LEN), f32)
     pairs = pltpu.VMEM((pixels, 2 * LIST_LEN), bf16)
     return pl.pallas_call(
@@ -825,10 +899,10 @@
         in_specs=[SMEM, VMEM, VMEM, VMEM],
         out_specs=VMEM,
         scratch_shapes=[
-            pltpu.VMEM((chunks, 8, LANES), f32),
+            pltpu.VMEM((max(chunks, tile_count), 8, LANES), f32),
             pltpu.VMEM((chunks, LANES), f32),
             pltpu.VMEM((tile_count, 16, LANES), f32),
-            pltpu.VMEM((batch, 48, LANES), f32),
+            pltpu.VMEM((BUFFERS * batch, 48, LANES), f32),
             plain,
             plain,
             plain,
@@ -837,8 +911,8 @@
             pairs,
             plain,
             pairs,
-            pltpu.VMEM((tile_count, 8, LANES), f32),
-            pltpu.VMEM((tile_count, LANES), f32),
+            pltpu.VMEM((ROWS * STRIDE, LANES), f32),
+            pltpu.VMEM((ROWS * tile_count, 3 * LANES), bf16),
             pltpu.VMEM((chunks, LANES), jnp.int32),
         ],
         compiler_params=pltpu.CompilerParams(vmem_limit_bytes=VMEM_LIMIT),
@@ -871,13 +945,15 @@
     forward = triangle_pair(True)
 
     def work(step):
-        first = step * batch
+        slot = (step % BUFFERS) * batch if isinstance(step, int) else 0
+        first = step * batch - slot
 
         def items(part):
-            return range(part * size, (part + 1) * size)
+            return range(slot + part * size, slot + (part + 1) * size)
 
         def span(part):
-            return slice(part * size * TILE_PIXELS, (part + 1) * size * TILE_PIXELS)
+            start = (slot + part * size) * TILE_PIXELS
+            return slice(start, start + size * TILE_PIXELS)
 
         def alphas(part):
             for item in items(part):
@@ -906,20 +982,17 @@
 
         staggered([alphas, befores, weights, colours], parts)
 
-    def batch_step(step, unused):
-        work(step - 1)
-        permute_group(lists_ref, main_ref, last_ref, chunks, step, write)
-        return unused
-
-    lax.fori_loop(1, tile_count // batch, batch_step, 0)
-    work(tile_count // batch - 1)
+    for step in range(tile_count // batch):
+        if step + 1 < tile_count // batch:
+            permute_group(lists_ref, main_ref, last_ref, chunks, step + 1, write)
+        work(step)
 
 
 def render(numbers, lists, packed):
     tile_count = lists.shape[0]
     chunks = packed.shape[0]
     batch = batch_tiles(tile_count)
-    pixels = batch * TILE_PIXELS
+    pixels = BUFFERS * batch * TILE_PIXELS
     plain = pltpu.VMEM((pixels, LIST_LEN), f32)
     pairs = pltpu.VMEM((pixels, 2 * LIST_LEN), bf16)
     return pl.pallas_call(
@@ -931,7 +1004,7 @@
             pltpu.VMEM((chunks, 8, LANES), f32),
             pltpu.VMEM((chunks, LANES), f32),
             pltpu.VMEM((tile_count, 16, LANES), f32),
-            pltpu.VMEM((batch, 48, LANES), f32),
+            pltpu.VMEM((BUFFERS * batch, 48, LANES), f32),
             plain,
             plain,
             pairs,
@@ -972,7 +1045,7 @@
     half_height = 0.5 * (lists_first.shape[0] * devices // TILES_X * tile_edge)
     keep = functools.partial(pltpu.with_memory_space_constraint, memory_space=pltpu.VMEM)
     leave = functools.partial(pltpu.with_memory_space_constraint, memory_space=pltpu.HBM)
-    packed = first_owner(
+    packed, kept_params = first_owner(
         leave(camera), leave(gauss_params), leave(send_first), half_width, half_height
     )
     packed = exchange(packed, devices)
@@ -980,7 +1053,7 @@
     packed = exchange(packed, devices)
     new_params, new_first, new_second, packed = second_owner(
         camera,
-        keep(gauss_params),
+        keep(kept_params),
         leave(adam_first),
         leave(adam_second),
         keep(send_first),

time: 70.8 us -> 65.1 us (0.919)
  Pallas kernels: 33.6 us -> 27.9 us
    pallas_call x1, Pallas kernels: 12.6 us -> 10.5 us  [train(): pl.pallas_call(train_body, out_shape=pltpu.VMEM(packed.shape, f32), in_sp...]
    pallas_call x1, Pallas kernels: 5.07 us -> 3.76 us  [first_owner(): pl.pallas_call(functools.partial(first_owner_body, half_width, half_heigh...]
    pallas_call x1, Pallas kernels: 10.4 us -> 9.21 us  [second_owner(): pl.pallas_call(functools.partial(second_owner_body, half_width, half_heig...]
    pallas_call x1, Pallas kernels: 5.56 us -> 4.47 us  [render(): pl.pallas_call(render_body, out_shape=jax.ShapeDtypeStruct((3, tile_count...]
where the time goes in v5:
time: 65.1 us; the launch traced here: 64.9 us
  blocking collectives  36.2 us (56%)
  Pallas kernels  27.9 us (43%)
  between operations  0.73 us (1%)
    all_to_all x3, blocking collectives, exchange(): lax.all_to_all(packed, 'dev', split_axis=0, concat_axis=0, tiled=True)  36.2 us
    pallas_call x1, Pallas kernels, train(): pl.pallas_call(train_body, out_shape=pltpu.VMEM(packed.shape, f32), in_sp...  10.5 us
    pallas_call x1, Pallas kernels, second_owner(): pl.pallas_call(functools.partial(second_owner_body, half_width, half_heig...  9.21 us
    pallas_call x1, Pallas kernels, render(): pl.pallas_call(render_body, out_shape=jax.ShapeDtypeStruct((3, tile_count...  4.47 us
    pallas_call x1, Pallas kernels, first_owner(): pl.pallas_call(functools.partial(first_owner_body, half_width, half_heigh...  3.76 us

profile of v5, /device:TPU:0, one launch (start us, length us, event | category | flops | bytes accessed | tf_op | source)
XLA Modules:
  0.0 64.9 jit_solution(9014196135556401869)
XLA Ops:
  0.6 0.0 copy-start.1
  0.6 0.0 copy-start.5
  0.7 0.0 copy-start
  0.7 0.0 copy-start.6
  0.7 0.0 copy-start.3
  0.7 0.0 copy-start.2
  0.7 3.8 %first_owner.1 = (f32[32,1,1152]{2,1,0:T(1,128)S(1)}, f32[59,8192]{1,0:T(8,128)S(1)}) custom-call(f32[2,6]{1,0:T(2,128)} %camera_ref.1, f32[59,8192]{1,0:T(8,128)} %params_hbm.1, s32[1,4096]{1,0:T(1,128)} %slots_ref.1), custom_call_target="tpu_custom_call" | custom-call | tf_op jit(solution)/shard_map/first_owner/pallas_call | solution.py:409
  4.5 15.5 %all_to_all.15.packed_ref = f32[32,1,1152]{2,1,0:T(1,128)S(1)} all-to-all(f32[32,1,1152]{2,1,0:T(1,128)S(1)} %get-tuple-element.11), channel_id=1, replica_groups=mesh['dev'=32] {'dev'}, dimensions={0} | all-to-all | bytes 294912 | tf_op jit(solution)/shard_map/all_to_all | solution.py:1021
  20.0 0.0 copy-done
  20.0 0.0 copy-done.6
  20.0 0.0 copy-done.3
  20.0 10.5 %train_tiles.1 = f32[32,1,1152]{2,1,0:T(1,128)S(1)} custom-call(s32[32]{0:T(128)S(1)} %copy-done.6, s32[32,128]{1,0:T(8,128)S(1)} %copy-done.3, f32[3,32,256]{2,1,0:T(8,128)S(1)} %bitcast.2, f32[32,1,1152]{2,1,0:T(1,128)S(1)} %all_to_all.15.packed_ref), custom_call_target="tpu_custom_call" | custom-call | tf_op jit(solution)/shard_map/train_tiles/pallas_call | solution.py:896
  30.5 10.3 %all_to_all.16.packed_ref = f32[32,1,1152]{2,1,0:T(1,128)S(1)} all-to-all(f32[32,1,1152]{2,1,0:T(1,128)S(1)} %train_tiles.1), channel_id=1, replica_groups=mesh['dev'=32] {'dev'}, dimensions={0} | all-to-all | bytes 294912 | tf_op jit(solution)/shard_map/all_to_all | solution.py:1021
  40.8 0.0 copy-done.1
  40.8 0.0 copy-done.5
  40.8 0.0 copy-done.2
  40.8 0.0 copy-start.4
  40.8 0.0 copy-start.7
  40.8 9.2 %second_owner.1 = (f32[59,8192]{1,0:T(8,128)}, f32[59,8192]{1,0:T(8,128)}, f32[59,8192]{1,0:T(8,128)}, f32[32,1,1152]{2,1,0:T(1,128)S(1)}) custom-call(f32[2,6]{1,0:T(2,128)S(1)} %copy-done.5, f32[59,8192]{1,0:T(8,128)S(1)} %get-tuple-element.10.params_ref, f32[59,8192]{1,0:T(8,128)} %first_hbm.1, f32[59,8192]{1,0:T(8,128)} %second_hbm.1, ...), custom_call_target="tpu_custom_call" | custom-call | tf_op jit(solution)/shard_map/second_owner/pallas_call | solution.py:579
  50.1 10.3 %all_to_all.17.packed_ref = f32[32,1,1152]{2,1,0:T(1,128)S(1)} all-to-all(f32[32,1,1152]{2,1,0:T(1,128)S(1)} %get-tuple-element.15), channel_id=1, replica_groups=mesh['dev'=32] {'dev'}, dimensions={0} | all-to-all | bytes 294912 | tf_op jit(solution)/shard_map/all_to_all | solution.py:1021
  60.4 0.0 copy-done.4
  60.4 0.0 copy-done.7
  60.4 4.5 %render_tiles.1 = f32[3,32,256]{2,1,0:T(8,128)} custom-call(s32[32]{0:T(128)S(1)} %copy-done.7, s32[32,128]{1,0:T(8,128)S(1)} %copy-done.4, f32[32,1,1152]{2,1,0:T(1,128)S(1)} %all_to_all.17.packed_ref), custom_call_target="tpu_custom_call" | custom-call | tf_op jit(solution)/shard_map/render_tiles/pallas_call | solution.py:998
Async XLA Ops:
  0.6 40.2 %copy-start.1 = (s32[1,4096]{1,0:T(1,128)S(1)}, s32[1,4096]{1,0:T(1,128)}, u32[]{:S(2)}) copy-start(s32[1,4096]{1,0:T(1,128)} %slots_ref.1) | copy-start | bytes 49156
  0.6 40.2 %copy-start.5 = (f32[2,6]{1,0:T(2,128)S(1)}, f32[2,6]{1,0:T(2,128)}, u32[]{:S(2)}) copy-start(f32[2,6]{1,0:T(2,128)} %camera_ref.1) | copy-start | bytes 148
  0.7 19.4 %copy-start = (f32[32,3,256]{2,0,1:T(8,128)S(1)}, f32[32,3,256]{2,0,1:T(8,128)}, u32[]{:S(2)}) copy-start(f32[32,3,256]{2,0,1:T(8,128)} %param.21) | copy-start | bytes 294916
  0.7 19.3 %copy-start.6 = (s32[32]{0:T(128)S(1)}, s32[32]{0:T(128)}, u32[]{:S(2)}) copy-start(s32[32]{0:T(128)} %numbers_ref.2) | copy-start | bytes 388
  0.7 19.3 %copy-start.3 = (s32[32,128]{1,0:T(8,128)S(1)}, s32[32,128]{1,0:T(8,128)}, u32[]{:S(2)}) copy-start(s32[32,128]{1,0:T(8,128)} %lists_ref.2) | copy-start | bytes 49156
  0.7 40.1 %copy-start.2 = (s32[1,4096]{1,0:T(1,128)S(1)}, s32[1,4096]{1,0:T(1,128)}, u32[]{:S(2)}) copy-start(s32[1,4096]{1,0:T(1,128)} %next_slots_ref.1) | copy-start | bytes 49156
  40.8 19.6 %copy-start.4 = (s32[32,128]{1,0:T(8,128)S(1)}, s32[32,128]{1,0:T(8,128)}, u32[]{:S(2)}) copy-start(s32[32,128]{1,0:T(8,128)} %lists_ref.3) | copy-start | bytes 49156
  40.8 19.6 %copy-start.7 = (s32[32]{0:T(128)S(1)}, s32[32]{0:T(128)}, u32[]{:S(2)}) copy-start(s32[32]{0:T(128)} %numbers_ref.3) | copy-start | bytes 388

commit v6 on v5

--- a/solution.py
+++ b/solution.py
@@ -434,7 +434,7 @@
     params_ref,
     first_hbm,
     second_hbm,
-    slots_ref,
+    inverse_ref,
     next_slots_ref,
     packed_ref,
     out_params_hbm,
@@ -450,7 +450,6 @@
     parts_ref,
     last_ref,
     idx_ref,
-    inverse_ref,
     first_ref,
     second_ref,
     params_out_ref,
@@ -460,7 +459,7 @@
     store_sems,
 ):
     chunks = params_ref.shape[1] // LANES
-    rows = slots_ref.shape[1] // LANES
+    rows = next_slots_ref.shape[1] // LANES
     groups = chunks // 8
 
     def columns_of(group):
@@ -480,8 +479,6 @@
     for group in range(groups):
         for copy in loads(group):
             copy.start()
-    slots_as_rows(slots_ref, idx_ref, rows)
-    invert(idx_ref, rows, chunks, inverse_ref)
     unpack(packed_ref, main_ref, last_ref, rows)
     frame = camera_frame(camera_ref, 0)
     next_frame = camera_frame(camera_ref, 1)
@@ -572,9 +569,9 @@
             copy.wait()
 
 
-def second_owner(camera, params, first, second, slots, next_slots, packed, half_width, half_height):
+def second_owner(camera, params, first, second, inverse, next_slots, packed, half_width, half_height):
     chunks = params.shape[1] // LANES
-    rows = slots.shape[1] // LANES
+    rows = next_slots.shape[1] // LANES
     shape = jax.ShapeDtypeStruct(params.shape, f32)
     return pl.pallas_call(
         functools.partial(second_owner_body, half_width, half_height),
@@ -591,7 +588,6 @@
             pltpu.VMEM((ROWS * chunks, 3 * LANES), bf16),
             pltpu.VMEM((rows, LANES), f32),
             pltpu.VMEM((rows, LANES), jnp.int32),
-            pltpu.VMEM((chunks, LANES), jnp.int32),
             pltpu.VMEM(params.shape, f32),
             pltpu.VMEM(params.shape, f32),
             pltpu.VMEM(params.shape, f32),
@@ -602,7 +598,30 @@
         ],
         compiler_params=pltpu.CompilerParams(vmem_limit_bytes=VMEM_LIMIT),
         name="second_owner",
-    )(camera, params, first, second, slots, next_slots, packed)
+    )(camera, params, first, second, inverse, next_slots, packed)
+
+
+def prepare_body(lists_ref, slots_ref, unused_ref, lists_inverse_ref, slots_inverse_ref, idx_ref):
+    rows = slots_ref.shape[1] // LANES
+    invert(lists_ref, lists_ref.shape[0], lists_inverse_ref.shape[0], lists_inverse_ref)
+    slots_as_rows(slots_ref, idx_ref, rows)
+    invert(idx_ref, rows, slots_inverse_ref.shape[0], slots_inverse_ref)
+
+
+def prepare(lists, slots, after, columns):
+    rows = slots.shape[1] // LANES
+    return pl.pallas_call(
+        prepare_body,
+        out_shape=(
+            pltpu.VMEM((rows, LANES), jnp.int32),
+            pltpu.VMEM((columns // LANES, LANES), jnp.int32),
+        ),
+        in_specs=[VMEM, VMEM, ANY],
+        out_specs=(VMEM, VMEM),
+        scratch_shapes=[pltpu.VMEM((rows, LANES), jnp.int32)],
+        compiler_params=pltpu.CompilerParams(vmem_limit_bytes=VMEM_LIMIT),
+        name="prepare",
+    )(lists, slots, after)
 
 
 def halves(value):
@@ -722,6 +741,7 @@
     lists_ref,
     targets_ref,
     packed_ref,
+    inverse_ref,
     out_packed_ref,
     main_ref,
     last_ref,
@@ -737,7 +757,6 @@
     grad_pair_ref,
     grad_ref,
     parts_ref,
-    inverse_ref,
 ):
     tile_count = lists_ref.shape[0]
     chunks = packed_ref.shape[0]
@@ -746,7 +765,6 @@
     size = batch // parts
     unpack(packed_ref, main_ref, last_ref, chunks)
     write = write_tiles(splat_ref)
-    invert(lists_ref, tile_count, chunks, inverse_ref)
     permute_group(lists_ref, main_ref, last_ref, chunks, 0, write)
     forward = triangle_pair(True)
     backward = triangle_pair(False)
@@ -874,19 +892,16 @@
 
         staggered([alphas, befores, weights, deltas, afters, moments], parts)
 
-    def batch_step(step, unused):
-        work(step - 1)
-        permute_group(lists_ref, main_ref, last_ref, chunks, step, write)
-        return unused
-
-    lax.fori_loop(1, tile_count // batch, batch_step, 0)
-    work(tile_count // batch - 1)
+    for step in range(tile_count // batch):
+        if step + 1 < tile_count // batch:
+            permute_group(lists_ref, main_ref, last_ref, chunks, step + 1, write)
+        work(step)
     send_splats(
         grad_ref, main_ref, parts_ref, inverse_ref, out_packed_ref, tile_count, chunks
     )
 
 
-def train(numbers, lists, targets, packed):
+def train(numbers, lists, targets, packed, inverse):
     tile_count = lists.shape[0]
     chunks = packed.shape[0]
     batch = batch_tiles(tile_count)
@@ -896,7 +911,7 @@
     return pl.pallas_call(
         train_body,
         out_shape=pltpu.VMEM(packed.shape, f32),
-        in_specs=[SMEM, VMEM, VMEM, VMEM],
+        in_specs=[SMEM, VMEM, VMEM, VMEM, VMEM],
         out_specs=VMEM,
         scratch_shapes=[
             pltpu.VMEM((max(chunks, tile_count), 8, LANES), f32),
@@ -913,11 +928,10 @@
             pairs,
             pltpu.VMEM((ROWS * STRIDE, LANES), f32),
             pltpu.VMEM((ROWS * tile_count, 3 * LANES), bf16),
-            pltpu.VMEM((chunks, LANES), jnp.int32),
         ],
         compiler_params=pltpu.CompilerParams(vmem_limit_bytes=VMEM_LIMIT),
         name="train_tiles",
-    )(numbers, lists, targets, packed)
+    )(numbers, lists, targets, packed, inverse)
 
 
 def render_body(
@@ -1049,14 +1063,19 @@
         leave(camera), leave(gauss_params), leave(send_first), half_width, half_height
     )
     packed = exchange(packed, devices)
-    packed = train(tiles_first, keep(lists_first), jnp.transpose(targets, (1, 0, 2)), packed)
+    lists_inverse, slots_inverse = prepare(
+        keep(lists_first), keep(send_first), kept_params, gauss_params.shape[1]
+    )
+    packed = train(
+        tiles_first, keep(lists_first), jnp.transpose(targets, (1, 0, 2)), packed, lists_inverse
+    )
     packed = exchange(packed, devices)
     new_params, new_first, new_second, packed = second_owner(
         camera,
         keep(kept_params),
         leave(adam_first),
         leave(adam_second),
-        keep(send_first),
+        keep(slots_inverse),
         keep(send_second),
         packed,
         half_width,

time: 65.1 us -> 64.1 us (0.985)
  blocking collectives: 36.2 us -> 20.7 us
  waiting for transfers between devices: 0 us -> 7.59 us
  starting transfers between devices: 0 us -> 7.34 us
    all_to_all x3 -> x2, blocking collectives: 36.2 us -> 20.7 us  [exchange(): lax.all_to_all(packed, 'dev', split_axis=0, concat_axis=0, tiled=True)]
    all_to_all x0 -> x1, waiting for transfers between devices: none -> 7.59 us  [exchange(): lax.all_to_all(packed, 'dev', split_axis=0, concat_axis=0, tiled=True)]
    all_to_all x0 -> x1, starting transfers between devices: none -> 7.34 us  [exchange(): lax.all_to_all(packed, 'dev', split_axis=0, concat_axis=0, tiled=True)]
    pallas_call x1, Pallas kernels: 10.5 us -> 9.23 us  [train(): pl.pallas_call(train_body, out_shape=pltpu.VMEM(packed.shape, f32), in_sp...]
    pallas_call x0 -> x1, Pallas kernels: none -> 0.8 us  [prepare(): pl.pallas_call(prepare_body, out_shape=(pltpu.VMEM((rows, LANES), jnp.int...]
    pallas_call x1, Pallas kernels: 9.21 us -> 8.51 us  [second_owner(): pl.pallas_call(functools.partial(second_owner_body, half_width, half_heig...]
    pallas_call x1, Pallas kernels: 3.76 us -> 4.41 us  [first_owner(): pl.pallas_call(functools.partial(first_owner_body, half_width, half_heigh...]
  transfers between devices with their start and end apart: 0 -> 1, of which waited for: 0 -> 1; matrix products, arithmetic and copies ran while one was open for 0% -> 0% of each run, Pallas kernels for 0% -> 1%
where the time goes in v6:
time: 64.1 us; the launch traced here: 63.8 us
  Pallas kernels  27.4 us (43%)
  blocking collectives  20.7 us (32%)
  waiting for transfers between devices  7.59 us (12%)
  starting transfers between devices  7.34 us (11%)
  between operations  0.74 us (1%)
    all_to_all x2, blocking collectives, exchange(): lax.all_to_all(packed, 'dev', split_axis=0, concat_axis=0, tiled=True)  20.7 us
    pallas_call x1, Pallas kernels, train(): pl.pallas_call(train_body, out_shape=pltpu.VMEM(packed.shape, f32), in_sp...  9.23 us
    pallas_call x1, Pallas kernels, second_owner(): pl.pallas_call(functools.partial(second_owner_body, half_width, half_heig...  8.51 us
    all_to_all x1, waiting for transfers between devices, exchange(): lax.all_to_all(packed, 'dev', split_axis=0, concat_axis=0, tiled=True)  7.59 us
    all_to_all x1, starting transfers between devices, exchange(): lax.all_to_all(packed, 'dev', split_axis=0, concat_axis=0, tiled=True)  7.34 us
    pallas_call x1, Pallas kernels, render(): pl.pallas_call(render_body, out_shape=jax.ShapeDtypeStruct((3, tile_count...  4.47 us
    pallas_call x1, Pallas kernels, first_owner(): pl.pallas_call(functools.partial(first_owner_body, half_width, half_heigh...  4.41 us
  transfers between devices with their start and end apart: 1, of which 1 were waited for; matrix products, arithmetic and copies ran while one was open for 0% of the time, Pallas kernels for 1%

profile of v6, /device:TPU:0, one launch (start us, length us, event | category | flops | bytes accessed | tf_op | source)
XLA Modules:
  0.0 63.8 jit_solution(5958844045643434631)
XLA Ops:
  0.6 0.0 copy-start.1
  0.6 0.0 copy-start.2
  0.7 0.0 copy-start
  0.7 0.0 copy-start.6
  0.7 4.4 %first_owner.1 = (f32[32,1,1152]{2,1,0:T(1,128)}, f32[59,8192]{1,0:T(8,128)S(1)}) custom-call(f32[2,6]{1,0:T(2,128)} %camera_ref.1, f32[59,8192]{1,0:T(8,128)} %params_hbm.1, s32[1,4096]{1,0:T(1,128)} %slots_ref.1), custom_call_target="tpu_custom_call" | custom-call | tf_op jit(solution)/shard_map/first_owner/pallas_call | solution.py:409
  5.1 0.0 copy-start.3
  5.1 0.0 copy-start.5
  5.1 7.3 %all-to-all-start = ((f32[32,1,1152]{2,1,0:T(1,128)}), f32[32,1,1152]{2,1,0:T(1,128)S(1)}, u32[]{:S(2)}, u32[]{:S(2)}) async-start(f32[32,1,1152]{2,1,0:T(1,128)} %get-tuple-element.14), calls=%async_computation | async-start | bytes 294912 | tf_op jit(solution)/shard_map/all_to_all | solution.py:1035
  12.5 0.0 copy-done.1
  12.5 0.0 copy-done.2
  12.5 0.8 %prepare.1 = (s32[32,128]{1,0:T(8,128)S(1)}, s32[64,128]{1,0:T(8,128)S(1)}) custom-call(s32[32,128]{1,0:T(8,128)S(1)} %copy-done.2, s32[1,4096]{1,0:T(1,128)S(1)} %copy-done.1, f32[59,8192]{1,0:T(8,128)S(1)} %get-tuple-element.12.unused_ref.params_ref), custom_call_target="tpu_custom_call" | custom-call | tf_op jit(solution)/shard_map/prepare/pallas_call | solution.py:613
  13.3 7.6 %all-to-all-done.packed_ref = f32[32,1,1152]{2,1,0:T(1,128)S(1)} async-done(((f32[32,1,1152]{2,1,0:T(1,128)}), f32[32,1,1152]{2,1,0:T(1,128)S(1)}, u32[]{:S(2)}, u32[]{:S(2)}) %all-to-all-start) | async-done | bytes 147488 | tf_op jit(solution)/shard_map/all_to_all | solution.py:1035
  20.9 0.0 copy-done
  20.9 0.0 copy-done.6
  20.9 9.2 %train_tiles.1 = f32[32,1,1152]{2,1,0:T(1,128)S(1)} custom-call(s32[32]{0:T(128)S(1)} %copy-done.6, s32[32,128]{1,0:T(8,128)S(1)} %copy-done.2, f32[3,32,256]{2,1,0:T(8,128)S(1)} %bitcast.2, f32[32,1,1152]{2,1,0:T(1,128)S(1)} %all-to-all-done.packed_ref, s32[32,128]{1,0:T(8,128)S(1)} %get-tuple-element.15.inverse_ref), custom_call_target="tpu_custom_call" | custom-call | tf_op jit(solution)/shard_map/train_tiles/pallas_call | solution.py:911
  30.1 10.3 %all_to_all.15.packed_ref = f32[32,1,1152]{2,1,0:T(1,128)S(1)} all-to-all(f32[32,1,1152]{2,1,0:T(1,128)S(1)} %train_tiles.1), channel_id=1, replica_groups=mesh['dev'=32] {'dev'}, dimensions={0} | all-to-all | bytes 294912 | tf_op jit(solution)/shard_map/all_to_all | solution.py:1035
  40.4 0.0 copy-done.3
  40.4 0.0 copy-done.5
  40.4 0.0 copy-start.4
  40.5 8.5 %second_owner.1 = (f32[59,8192]{1,0:T(8,128)}, f32[59,8192]{1,0:T(8,128)}, f32[59,8192]{1,0:T(8,128)}, f32[32,1,1152]{2,1,0:T(1,128)S(1)}) custom-call(f32[2,6]{1,0:T(2,128)S(1)} %copy-done.5, f32[59,8192]{1,0:T(8,128)S(1)} %get-tuple-element.12.unused_ref.params_ref, f32[59,8192]{1,0:T(8,128)} %first_hbm.1, f32[59,8192]{1,0:T(8,128)} %second_hbm.1, ...), custom_call_target="tpu_custom_call" | custom-call | tf_op jit(solution)/shard_map/second_owner/pallas_call | solution.py:576
  49.0 10.3 %all_to_all.16.packed_ref = f32[32,1,1152]{2,1,0:T(1,128)S(1)} all-to-all(f32[32,1,1152]{2,1,0:T(1,128)S(1)} %get-tuple-element.19), channel_id=1, replica_groups=mesh['dev'=32] {'dev'}, dimensions={0} | all-to-all | bytes 294912 | tf_op jit(solution)/shard_map/all_to_all | solution.py:1035
  59.3 0.0 copy-done.4
  59.3 0.0 copy-done.7
  59.3 4.5 %render_tiles.1 = f32[3,32,256]{2,1,0:T(8,128)} custom-call(s32[32]{0:T(128)S(1)} %copy-done.7, s32[32,128]{1,0:T(8,128)S(1)} %copy-done.4, f32[32,1,1152]{2,1,0:T(1,128)S(1)} %all_to_all.16.packed_ref), custom_call_target="tpu_custom_call" | custom-call | tf_op jit(solution)/shard_map/render_tiles/pallas_call | solution.py:1012
  (1 shorter events, 0.0 us)
Async XLA Ops:
  0.6 11.8 %copy-start.1 = (s32[1,4096]{1,0:T(1,128)S(1)}, s32[1,4096]{1,0:T(1,128)}, u32[]{:S(2)}) copy-start(s32[1,4096]{1,0:T(1,128)} %slots_ref.1) | copy-start | bytes 49156
  0.6 11.8 %copy-start.2 = (s32[32,128]{1,0:T(8,128)S(1)}, s32[32,128]{1,0:T(8,128)}, u32[]{:S(2)}) copy-start(s32[32,128]{1,0:T(8,128)} %lists_ref.4) | copy-start | bytes 49156
  0.7 20.2 %copy-start = (f32[32,3,256]{2,0,1:T(8,128)S(1)}, f32[32,3,256]{2,0,1:T(8,128)}, u32[]{:S(2)}) copy-start(f32[32,3,256]{2,0,1:T(8,128)} %param.21) | copy-start | bytes 294916
  0.7 20.2 %copy-start.6 = (s32[32]{0:T(128)S(1)}, s32[32]{0:T(128)}, u32[]{:S(2)}) copy-start(s32[32]{0:T(128)} %numbers_ref.2) | copy-start | bytes 388
  5.1 35.4 %copy-start.3 = (s32[1,4096]{1,0:T(1,128)S(1)}, s32[1,4096]{1,0:T(1,128)}, u32[]{:S(2)}) copy-start(s32[1,4096]{1,0:T(1,128)} %next_slots_ref.1) | copy-start | bytes 49156
  5.1 35.3 %copy-start.5 = (f32[2,6]{1,0:T(2,128)S(1)}, f32[2,6]{1,0:T(2,128)}, u32[]{:S(2)}) copy-start(f32[2,6]{1,0:T(2,128)} %camera_ref.1) | copy-start | bytes 148
  5.1 15.8 %all-to-all-start = ((f32[32,1,1152]{2,1,0:T(1,128)}), f32[32,1,1152]{2,1,0:T(1,128)S(1)}, u32[]{:S(2)}, u32[]{:S(2)}) async-start(f32[32,1,1152]{2,1,0:T(1,128)} %get-tuple-element.14), calls=%async_computation | async-start | bytes 294912 | tf_op jit(solution)/shard_map/all_to_all | solution.py:1035
  40.4 18.9 %copy-start.4 = (s32[32,128]{1,0:T(8,128)S(1)}, s32[32,128]{1,0:T(8,128)}, u32[]{:S(2)}) copy-start(s32[32,128]{1,0:T(8,128)} %lists_ref.5) | copy-start | bytes 49156
  40.4 18.9 %copy-start.7 = (s32[32]{0:T(128)S(1)}, s32[32]{0:T(128)}, u32[]{:S(2)}) copy-start(s32[32]{0:T(128)} %numbers_ref.3) | copy-start | bytes 388
